TPU v7x, 32 devices: a whole 2x2x4 slice. The times are simulated.
32 devices in a mesh: sub: 8 (over z, core), sta: 4 (over y, x).
Axes of the slice: x: 2, y: 2, z: 4, core: 2. Of those that a mesh axis runs over, the one named last changes fastest.
Arguments:
- voltages: bfloat16 [8, 2, 64, 65536], P('sub', None, 'sta'), may hold values from -6 to 6
- beam_weights: bfloat16 [8, 2, 32, 64], P('sub'), may hold values from -0.5 to 0.5
- station_delays: int32 [64], P('sta'), may hold values from 0 to 16383
- dm_index: int32 [32, 1], P('sta'), may hold values from 1 to 8
Outputs:
- dedispersed: float32 [8, 2, 32, 1, 65536], P(None, None, None, None, ('sub', 'sta'))
- intensity: float32 [32, 1, 65536], P(None, None, ('sub', 'sta'))
Inputs may be any that keep to these rules, and one draw needn't show every extreme that they name: `station_delays`: delays in whole samples. `dm_index`: dispersion measure in steps of 10.
All inputs are finite; a program needn't handle non-finite values.
Results may differ from a plain program's by a relative error of at most 0.0006.
Values may be sent and summed in bfloat16 or wider, within the bound.
A program may use at most 320 MiB of HBM per device.

v0:
```python
import functools

import jax
import jax.numpy as jnp
import numpy as np
from jax import lax
from jax.experimental import pallas as pl
from jax.experimental.pallas import tpu as pltpu
from jax.sharding import PartitionSpec as P


TWO_PI = 6.283185307179586
DISPERSION = 4148808000.0
DM_STEP = 10.0
BASE_FREQ = 120.0
CHANNEL_WIDTH = 0.1953125


def dft_tables(root_len):
    total_len = root_len * root_len
    product = np.outer(np.arange(root_len), np.arange(root_len))
    root_angle = 2 * np.pi * (product % root_len) / root_len
    cos_root, sin_root = np.cos(root_angle), np.sin(root_angle)
    left = np.block([[cos_root, sin_root], [-sin_root, cos_root]]).astype(np.float32)
    high = left.astype(jnp.bfloat16)
    low = (left - high.astype(np.float32)).astype(jnp.bfloat16)
    twist_angle = 2 * np.pi * product / total_len
    twist = np.stack([np.cos(twist_angle), np.sin(twist_angle)]).astype(np.float32)
    return np.stack([high, low]), np.stack([high.T, low.T]), twist


def chirp_base(subband, root_len, total_len):
    first = jnp.arange(root_len, dtype=jnp.int32)[:, None]
    second = jnp.arange(root_len, dtype=jnp.int32)[None, :]
    positions = first + root_len * second
    signed_bin = jnp.where(positions < total_len // 2, positions, positions - total_len)
    offset = (CHANNEL_WIDTH * signed_bin.astype(jnp.float32) / total_len)[None]
    centre = (BASE_FREQ + CHANNEL_WIDTH * (subband.astype(jnp.float32) + 0.5))[:, None, None]
    return TWO_PI * DISPERSION * offset * offset / (centre * centre * (centre + offset))


def beam_kernel(w_ref, v_ref, out_ref):
    sums = jnp.dot(w_ref[...], v_ref[...], preferred_element_type=jnp.float32)
    lanes = out_ref.shape[2]
    for row in range(out_ref.shape[1]):
        out_ref[:, row, :] = sums[:, row * lanes : (row + 1) * lanes]


def form_beams(weights, volts, root_len):
    rows, depth = weights.shape
    total_len = volts.shape[1]
    step = 32
    return pl.pallas_call(
        beam_kernel,
        grid=(root_len // step,),
        in_specs=[
            pl.BlockSpec((rows, depth), lambda i: (0, 0)),
            pl.BlockSpec((depth, step * root_len), lambda i: (0, i)),
        ],
        out_specs=pl.BlockSpec((rows, step, root_len), lambda i: (0, i, 0)),
        out_shape=jax.ShapeDtypeStruct((rows, root_len, root_len), jnp.float32),
        cost_estimate=pl.CostEstimate(
            flops=2 * rows * depth * total_len, bytes_accessed=2 * depth * total_len, transcendentals=0
        ),
    )(weights, volts)


def shift_kernel(delay_ref, x_ref, out_ref, doubled, window):
    rows, total_len = x_ref.shape[1:]
    width = window.shape[1]
    step = width - 128
    doubled[:, :total_len] = x_ref[0].astype(jnp.float32)
    doubled[:, total_len:] = doubled[:, :total_len]
    row_id = lax.broadcasted_iota(jnp.int32, (rows, width), 0)
    fine = jnp.zeros((rows, width), jnp.int32)
    for row in range(rows):
        fine = jnp.where(row_id == row, delay_ref[row] % 128, fine)

    def chunk(i, carry):
        for row in range(rows):
            start = total_len + i * step - (delay_ref[row] // 128) * 128 - 128
            window[row : row + 1, :] = doubled[row : row + 1, pl.ds(pl.multiple_of(start, 128), width)]
        values = window[...]
        for bit in range(7):
            values = jnp.where((fine >> bit) & 1 == 1, pltpu.roll(values, 1 << bit, 1), values)
        out_ref[0, :, pl.ds(pl.multiple_of(i * step, 128), step)] = values[:, 128:].astype(out_ref.dtype)
        return carry

    lax.fori_loop(0, total_len // step, chunk, 0)


def shift(volts, delays):
    parts, rows, total_len = volts.shape
    block = pl.BlockSpec((1, rows, total_len), lambda i: (i, 0, 0))
    return pl.pallas_call(
        shift_kernel,
        grid=(parts,),
        in_specs=[pl.BlockSpec(memory_space=pltpu.SMEM), block],
        out_specs=block,
        out_shape=jax.ShapeDtypeStruct(volts.shape, volts.dtype),
        scratch_shapes=[
            pltpu.VMEM((rows, 2 * total_len), jnp.float32),
            pltpu.VMEM((rows, 2048 + 128), jnp.float32),
        ],
    )(delays, volts)


def split(values):
    high = values.astype(jnp.bfloat16)
    return high, (values - high.astype(jnp.float32)).astype(jnp.bfloat16)


def dot3(a_high, a_low, b_high, b_low):
    dot = functools.partial(jnp.dot, preferred_element_type=jnp.float32)
    return dot(a_high, b_high) + (dot(a_high, b_low) + dot(a_low, b_high))


def dedisperse_kernel(x_ref, h_real_ref, h_imag_ref, left_ref, right_ref, twist_ref, out_ref, flat):
    root = twist_ref.shape[1]
    half = root // 2
    cos_twist, sin_twist = twist_ref[0], twist_ref[1]
    x = x_ref[...].reshape(2 * root, root)
    a = dot3(left_ref[0], left_ref[1], *split(x))
    a_real, a_imag = a[:root], a[root:]
    b = jnp.concatenate(
        [a_real * cos_twist + a_imag * sin_twist, a_imag * cos_twist - a_real * sin_twist], axis=1
    )
    s = dot3(*split(b), right_ref[0], right_ref[1])
    s_real, s_imag = s[:, :root], s[:, root:]
    h_real, h_imag = h_real_ref[0], h_imag_ref[0]
    c = jnp.concatenate([s_real * h_real - s_imag * h_imag, s_real * h_imag + s_imag * h_real], axis=1)
    d = dot3(*split(c), left_ref[0], left_ref[1])
    d_real, d_imag = d[:, :root], d[:, root:]
    e = jnp.concatenate(
        [d_real * cos_twist - d_imag * sin_twist, d_imag * cos_twist + d_real * sin_twist], axis=0
    )
    out = dot3(right_ref[0], right_ref[1], *split(e)) * (1.0 / (root * root))
    for part in range(2):
        for side in range(2):
            flat[pl.ds(side, root, 2), :] = out[part * root : (part + 1) * root, side * half : (side + 1) * half]
        out_ref[:, part, 0] = flat[...].reshape(out_ref.shape[0], out_ref.shape[3], half)


def dedisperse(beams, h_real, h_imag, n_dev):
    _, n_beams, root, _ = beams.shape
    left, right, twist = dft_tables(root)
    rows = 2 * root // n_dev
    whole = lambda shape: pl.BlockSpec(shape, lambda b: (0,) * len(shape))
    own = pl.BlockSpec((1, root, root), lambda b: (b, 0, 0))
    return pl.pallas_call(
        dedisperse_kernel,
        grid=(n_beams,),
        in_specs=[
            pl.BlockSpec((2, 1, root, root), lambda b: (0, b, 0, 0)),
            own,
            own,
            whole(left.shape),
            whole(right.shape),
            whole(twist.shape),
        ],
        out_specs=pl.BlockSpec((n_dev, 2, 1, rows, root // 2), lambda b: (0, 0, b, 0, 0)),
        out_shape=jax.ShapeDtypeStruct((n_dev, 2, n_beams, rows, root // 2), jnp.float32),
        scratch_shapes=[pltpu.VMEM((2 * root, root // 2), jnp.float32)],
        cost_estimate=pl.CostEstimate(
            flops=96 * n_beams * root**3, bytes_accessed=24 * n_beams * root**2, transcendentals=0
        ),
    )(beams, h_real, h_imag, left, right, twist)


def shards(voltages, beam_weights, station_delays, dm_index):
    sub_dev = voltages.shape[0]
    total_len = voltages.shape[3]
    local_beams = dm_index.shape[0]
    trials = dm_index.shape[1]
    root_len = int(round(total_len**0.5))
    n_sub = lax.axis_size("sub")
    n_sta = lax.axis_size("sta")
    n_dev = n_sub * n_sta
    assert sub_dev == 1 and trials == 1 and root_len * root_len == total_len
    shifted = shift(voltages[0], station_delays)
    own_weights = lax.dynamic_slice_in_dim(
        beam_weights, lax.axis_index("sta") * local_beams, local_beams, 2
    )[0]
    w_real, w_imag = own_weights[0], own_weights[1]
    volts = lax.all_gather(shifted, "sta", axis=1, tiled=True)
    volts = volts.reshape(-1, total_len)
    weights = jnp.concatenate(
        [jnp.concatenate([w_real, -w_imag], axis=1), jnp.concatenate([w_imag, w_real], axis=1)], axis=0
    )
    beams = form_beams(weights, volts, root_len).reshape(2, local_beams, root_len, root_len)
    subband = lax.axis_index("sub") + jnp.arange(1, dtype=jnp.int32)
    base_phase = chirp_base(subband, root_len, total_len)
    dm_value = DM_STEP * dm_index.astype(jnp.float32)
    phase_table = dm_value[:, :, None] * base_phase
    sent = dedisperse(beams, jnp.cos(phase_table), jnp.sin(phase_table), n_dev)
    power = jnp.mean(beams[0] * beams[0] + beams[1] * beams[1], axis=(1, 2))
    rms = jnp.where(power > 0, jnp.sqrt(power), 1.0)
    gain = 32768.0 / root_len / rms
    undo = lax.all_gather(rms * (root_len / 32768.0), ("sub", "sta"), axis=0)
    sent = (sent * gain[None, None, :, None, None]).astype(jnp.float16)
    moved = lax.all_to_all(sent, ("sub", "sta"), split_axis=0, concat_axis=0, tiled=True)
    moved = moved.astype(jnp.float32) * undo[:, None, :, None, None]
    moved = moved.reshape(n_sub, n_sta, *moved.shape[1:]).transpose(0, 2, 1, 3, 4, 5)
    moved = moved.reshape(n_sub, 2, n_sta * local_beams, *moved.shape[4:])
    intensity = jnp.mean(moved[:, 0] * moved[:, 0] + moved[:, 1] * moved[:, 1], axis=0)
    return (moved.reshape(*moved.shape[:3], 1, -1), intensity.reshape(intensity.shape[0], 1, -1))


def solution(mesh):
    return jax.shard_map(
        shards,
        mesh=mesh,
        in_specs=(
            P("sub", None, "sta", None),
            P("sub", None, None, None),
            P("sta"),
            P("sta", None),
        ),
        out_specs=(P(None, None, None, None, ("sub", "sta")), P(None, None, ("sub", "sta"))),
        check_vma=False,
    )
```

profile of v0, /device:TPU:0, one launch (start us, length us, event | category | flops | bytes accessed | tf_op | source)
XLA Modules:
  0.0 347.7 jit_solution(12698283413154339033)
XLA Ops:
  7.2 0.0 all-gather.3.cloned.1.call-start
  7.2 50.8 %shard_map.86 = bf16[2,16,65536]{2,1,0:T(8,128)(2,1)} custom-call(s32[16]{0:T(128)} %delay_ref.1, bf16[2,16,65536]{2,1,0:T(8,128)(2,1)} %bitcast.22), custom_call_target="tpu_custom_call" | custom-call | tf_op jit(solution)/shard_map/pallas_call | solution.py:95
  58.1 0.0 copy-start.1
  58.1 0.0 all-gather.3.cloned.1.call-update
  58.1 0.7 dynamic-slice_bitcast_fusion.1
  58.8 0.7 fusion.5
  59.5 0.7 maximum_maximum_fusion.w_ref
  60.2 0.0 copy-done.1
  60.2 0.1 multiply_divide_fusion
  60.3 8.8 %multiply_sine_fusion = (f32[8,256,256]{2,1,0:T(8,128)}, f32[8,256,256]{2,1,0:T(8,128)}) fusion(f32[256,256]{1,0:T(8,128)S(1)} %multiply_divide_fusion, f32[8]{0:T(128)S(1)} %multiply_bitcast_fusion), kind=kLoop, calls=%fused_computation.2 | loop fusion | flops 524288 | bytes 4456480 | tf_op jit(solution)/shard_map/sin | solution.py:195
  69.1 149.3 %all-gather.3.cloned.1.call-done = bf16[2,64,65536]{2,1,0:T(8,128)(2,1)} async-done(((bf16[2,16,65536]{2,1,0:T(8,128)(2,1)}), bf16[2,64,65536]{2,1,0:T(8,128)(2,1)}) %all-gather.3.cloned.1.call-update) | async-done | bytes 16777232 | tf_op jit(solution)/shard_map/all_gather | solution.py:185
  218.3 10.8 %shard_map.87 = f32[16,256,256]{2,1,0:T(8,128)} custom-call(bf16[16,128]{1,0:T(8,128)(2,1)} %maximum_maximum_fusion.w_ref, bf16[128,65536]{1,0:T(8,128)(2,1)} %bitcast.17), custom_call_target="tpu_custom_call" | custom-call | flops 268435456 | bytes 16777216 | tf_op jit(solution)/shard_map/pallas_call | solution.py:53
  229.1 2.6 fusion.3
  231.8 0.1 multiply_dynamic-update-slice_fusion
  231.9 26.7 %shard_map.88 = f32[32,2,8,16,128]{4,3,2,1,0:T(8,128)} custom-call(f32[2,8,256,256]{3,2,1,0:T(8,128)} %bitcast.21, f32[8,256,256]{2,1,0:T(8,128)} %get-tuple-element.7.h_real_ref, f32[8,256,256]{2,1,0:T(8,128)} %get-tuple-element.6.h_imag_ref, bf16[2,512,512]{2,1,0:T(8,128)(2,1)} %constant.62.clone.left_ref, bf16[2,512,512]{2,1,0:T(8,128)(2,1)} %constant.63.clone.right_ref, ...), custom_call_target="tpu_custom_call" | custom-call | flops 12884901888 | bytes 12582912 | tf_op jit(solution)/shard_map/pallas_call | solution.py:150
  258.6 4.2 %multiply_convert_fusion = f16[32,2,8,16,128]{4,3,2,1,0:T(8,128)(2,1)} fusion(f32[32,2,8,16,128]{4,3,2,1,0:T(8,128)} %shard_map.88, f32[8]{0:T(128)S(1)} %get-tuple-element.9), kind=kLoop, calls=%fused_computation.1 | loop fusion | flops 2097152 | bytes 6291488 | tf_op jit(solution)/shard_map/convert_element_type | solution.py:200
  262.8 4.6 %all-to-all-start = ((f16[32,2,8,16,128]{4,3,2,1,0:T(8,128)(2,1)}), f16[32,2,8,16,128]{4,3,2,1,0:T(8,128)(2,1)S(1)}, u32[]{:S(2)}, u32[]{:S(2)}) async-start(f16[32,2,8,16,128]{4,3,2,1,0:T(8,128)(2,1)} %multiply_convert_fusion), calls=%async_computation | async-start | bytes 4194304 | tf_op jit(solution)/shard_map/all_to_all | solution.py:201
  267.4 69.7 %all-reduce = f32[256]{0:T(256)S(1)} all-reduce(f32[256]{0:T(256)S(1)} %get-tuple-element.8), channel_id=2, replica_groups=mesh['sub'=8,'sta'=4] {'sub','sta'}, use_global_device_ids=true, to_apply=%add | all-reduce | flops 256 | bytes 2048
  337.1 0.1 reshape.138
  337.1 0.0 all-to-all-done
  337.1 0.4 convert_multiply_fusion
  337.6 0.5 copy.10
  338.1 0.0 copy-start
  338.1 0.3 fusion.1
  338.4 1.7 copy-done
  340.1 0.7 broadcast_multiply_fusion
  (3 shorter events, 0.0 us)
Async XLA Ops:
  7.2 211.2 %all-gather.3.cloned.1.call-start = ((), (), s32[]{:S(2)}) async-start(), calls=%async_computation.1 | async-start | bytes 20971520 | tf_op jit(solution)/shard_map/all_gather | solution.py:185
  58.1 2.1 copy-start.1
  262.8 74.4 %all-to-all-start = ((f16[32,2,8,16,128]{4,3,2,1,0:T(8,128)(2,1)}), f16[32,2,8,16,128]{4,3,2,1,0:T(8,128)(2,1)S(1)}, u32[]{:S(2)}, u32[]{:S(2)}) async-start(f16[32,2,8,16,128]{4,3,2,1,0:T(8,128)(2,1)} %multiply_convert_fusion), calls=%async_computation | async-start | bytes 4194304 | tf_op jit(solution)/shard_map/all_to_all | solution.py:201
  338.1 2.0 copy-start
Sparse Core Ops, SparseCore 0:
  58.2 160.0 all-gather.2
where the time goes:
time: 348 us
  waiting for transfers between devices  149 us (43%)
  Pallas kernels  88.4 us (25%)
  blocking collectives  69.7 us (20%)
  other arithmetic  18.6 us (5%)
  between operations  14.1 us (4%)
  starting transfers between devices  4.64 us (1%)
    all_gather x1, waiting for transfers between devices, shards(): volts = lax.all_gather(shifted, 'sta', axis=1, tiled=True)  149 us
    unnamed x1, blocking collectives  69.7 us
    pallas_call x1, Pallas kernels, shift(): pl.pallas_call(shift_kernel, grid=(parts,), in_specs=[pl.BlockSpec(memory...  50.8 us
    pallas_call x1, Pallas kernels, dedisperse(): pl.pallas_call(dedisperse_kernel, grid=(n_beams,), in_specs=[pl.BlockSpec...  26.7 us
    pallas_call x1, Pallas kernels, form_beams(): pl.pallas_call(beam_kernel, grid=(root_len // step,), in_specs=[pl.BlockS...  10.8 us
    sin x1, other arithmetic, shards(): sent = dedisperse(beams, jnp.cos(phase_table), jnp.sin(phase_table), n_dev)  8.79 us
  transfers between devices with their start and end apart: 2, of which 1 were waited for; matrix products, arithmetic and copies ran while one was open for 3% of the time, Pallas kernels for 0%

commit v1 on v0

--- a/solution.py
+++ b/solution.py
@@ -39,70 +39,264 @@
     return TWO_PI * DISPERSION * offset * offset / (centre * centre * (centre + offset))
 
 
-def beam_kernel(w_ref, v_ref, out_ref):
-    sums = jnp.dot(w_ref[...], v_ref[...], preferred_element_type=jnp.float32)
-    lanes = out_ref.shape[2]
-    for row in range(out_ref.shape[1]):
-        out_ref[:, row, :] = sums[:, row * lanes : (row + 1) * lanes]
-
-
-def form_beams(weights, volts, root_len):
-    rows, depth = weights.shape
-    total_len = volts.shape[1]
-    step = 32
-    return pl.pallas_call(
-        beam_kernel,
-        grid=(root_len // step,),
-        in_specs=[
-            pl.BlockSpec((rows, depth), lambda i: (0, 0)),
-            pl.BlockSpec((depth, step * root_len), lambda i: (0, i)),
-        ],
-        out_specs=pl.BlockSpec((rows, step, root_len), lambda i: (0, i, 0)),
-        out_shape=jax.ShapeDtypeStruct((rows, root_len, root_len), jnp.float32),
-        cost_estimate=pl.CostEstimate(
-            flops=2 * rows * depth * total_len, bytes_accessed=2 * depth * total_len, transcendentals=0
-        ),
-    )(weights, volts)
-
-
-def shift_kernel(delay_ref, x_ref, out_ref, doubled, window):
+def shift_kernel(delay_ref, x_ref, out_ref, source, moved):
     rows, total_len = x_ref.shape[1:]
-    width = window.shape[1]
-    step = width - 128
-    doubled[:, :total_len] = x_ref[0].astype(jnp.float32)
-    doubled[:, total_len:] = doubled[:, :total_len]
-    row_id = lax.broadcasted_iota(jnp.int32, (rows, width), 0)
-    fine = jnp.zeros((rows, width), jnp.int32)
+    blocks = total_len // 128
+    pitch = source.shape[0] // (blocks + 16)
+    def load(i, carry):
+        for u in range(8):
+            j = i * 8 + u
+            source[pl.ds(j*pitch, rows), :] = x_ref[0, :, pl.ds(pl.multiple_of(j * 128, 128), 128)].astype(jnp.float32)
+        return carry
+    lax.fori_loop(0, blocks // 8, load, 0)
+    for u in range(16):
+        source[pl.ds((blocks + u) * pitch, rows), :] = source[pl.ds(u * pitch, rows), :]
+    lane = lax.broadcasted_iota(jnp.int32, (8, 128), 1)
     for row in range(rows):
-        fine = jnp.where(row_id == row, delay_ref[row] % 128, fine)
-
-    def chunk(i, carry):
-        for row in range(rows):
-            start = total_len + i * step - (delay_ref[row] // 128) * 128 - 128
-            window[row : row + 1, :] = doubled[row : row + 1, pl.ds(pl.multiple_of(start, 128), width)]
-        values = window[...]
-        for bit in range(7):
-            values = jnp.where((fine >> bit) & 1 == 1, pltpu.roll(values, 1 << bit, 1), values)
-        out_ref[0, :, pl.ds(pl.multiple_of(i * step, 128), step)] = values[:, 128:].astype(out_ref.dtype)
+        delay = delay_ref[row]
+        fine = delay & 127
+        coarse = delay >> 7
+        keep = lane < 128 - fine
+        def chunk(i, carry):
+            for u in range(32):
+                j = i * (8*32) + u * 8
+                start = (j - coarse - 1) & (blocks - 1)
+                before = source[pl.ds(start * pitch + row, 8, stride=pitch), :]
+                after = source[pl.ds((start + 1) * pitch + row, 8, stride=pitch), :]
+                values = pltpu.roll(jnp.where(keep, after, before), fine, 1)
+                moved[pl.ds(j * pitch + row, 8, stride=pitch), :] = values
+            return carry
+        lax.fori_loop(0, blocks // (8*32), chunk, 0)
+    def store(i, carry):
+        for u in range(8):
+            j = i * 8 + u
+            out_ref[j] = moved[pl.ds(j*pitch, rows), :].astype(out_ref.dtype)
         return carry
-
-    lax.fori_loop(0, total_len // step, chunk, 0)
+    lax.fori_loop(0, blocks // 8, store, 0)
 
 
 def shift(volts, delays):
     parts, rows, total_len = volts.shape
-    block = pl.BlockSpec((1, rows, total_len), lambda i: (i, 0, 0))
+    blocks = total_len // 128
+    pitch = rows + 4
     return pl.pallas_call(
         shift_kernel,
         grid=(parts,),
-        in_specs=[pl.BlockSpec(memory_space=pltpu.SMEM), block],
-        out_specs=block,
-        out_shape=jax.ShapeDtypeStruct(volts.shape, volts.dtype),
+        in_specs=[pl.BlockSpec(memory_space=pltpu.SMEM), pl.BlockSpec((1, rows, total_len), lambda i: (i, 0, 0))],
+        out_specs=pl.BlockSpec((blocks, rows, 128), lambda i: (0, i, 0)),
+        out_shape=jax.ShapeDtypeStruct((blocks, parts * rows, 128), volts.dtype),
+        scratch_shapes=[pltpu.VMEM(((blocks + 16) * pitch, 128), jnp.float32), pltpu.VMEM((blocks * pitch, 128), jnp.float32)],
+    )(delays, volts)
+
+
+MESH = pl.DeviceIdType.MESH
+PEAK = 32767.0
+
+
+def peers(side, n_low, n_high):
+    sub, sta = lax.axis_index("sub"), lax.axis_index("sta")
+    high, low = sta // n_low, lax.rem(sta, n_low)
+    along = (
+        [(sub, high * n_low + lax.rem(low + k, n_low)) for k in range(1, n_low)],
+        [(sub, lax.rem(high + k, n_high) * n_low + low) for k in range(1, n_high)],
+    )
+    return along[side], along[1 - side]
+
+
+def quantize(values, ceiling):
+    return jnp.round(values * (PEAK / jnp.maximum(ceiling, 1e-30))).astype(jnp.int32).astype(jnp.int16)
+
+
+def dequantize(codes, ceiling):
+    return codes.astype(jnp.int32).astype(jnp.float32) * (ceiling * (1.0 / PEAK))
+
+
+def beams_kernel(n_low, n_high, chunks, volt_ref, w0_ref, w1_ref, out_ref, *scratch):
+    got, partial, codes, landed, scale, scale_in = (scratch[2 * i : 2 * i + 2] for i in range(6))
+    gather_send, gather_recv, sum_send, sum_recv, scale_send, scale_recv = (
+        scratch[12 + 2 * i : 14 + 2 * i] for i in range(6)
+    )
+    weight_refs = (w0_ref, w1_ref)
+    n_beams, root = out_ref.shape[1:3]
+    half = root // 2
+    pitch = partial[0].shape[1] // weight_refs[0].shape[0]
+    blocks = volt_ref.shape[0] // 2 // chunks
+
+    barrier = pltpu.get_barrier_semaphore()
+    for peer in (*peers(0, n_low, n_high)[0], *peers(0, n_low, n_high)[1]):
+        pl.semaphore_signal(barrier, inc=1, device_id=peer, device_id_type=MESH)
+    pl.semaphore_wait(barrier, n_low + n_high - 2)
+
+    gathers = {}
+    for chunk in range(chunks):
+        for side in range(2):
+            for k, peer in enumerate(peers(side, n_low, n_high)[0]):
+                copy = pltpu.make_async_remote_copy(
+                    src_ref=volt_ref.at[pl.ds((side * chunks + chunk) * blocks, blocks)],
+                    dst_ref=got[side].at[k, pl.ds(chunk * blocks, blocks)],
+                    send_sem=gather_send[side].at[k, chunk],
+                    recv_sem=gather_recv[side].at[k, chunk],
+                    device_id=peer,
+                    device_id_type=MESH,
+                )
+                copy.start()
+                gathers[side, k, chunk] = copy
+
+    for chunk in range(chunks):
+        for side in range(2):
+            members = len(peers(side, n_low, n_high)[0])
+            for k in range(members):
+                gathers[side, k, chunk].wait_recv()
+            weights = weight_refs[side][...]
+
+            def rows(i, carry):
+                for u in range(8):
+                    row = chunk * (blocks // 2) + i * 8 + u
+                    own = side * (volt_ref.shape[0] // 2) + 2 * row
+                    tall = [
+                        jnp.concatenate([ref[at], ref[at + 1]], axis=1)
+                        for ref, at in ((volt_ref, own), *((got[side].at[k], 2 * row) for k in range(members)))
+                    ]
+                    sums = jnp.dot(weights, jnp.concatenate(tall, axis=0), preferred_element_type=jnp.float32)
+                    for lanes in range(2):
+                        for base in range(0, weights.shape[0], 8):
+                            partial[side][lanes, pl.ds(base * pitch + row, 8, stride=pitch), :] = sums[
+                                base : base + 8, lanes * 128 : (lanes + 1) * 128
+                            ]
+                return carry
+
+            lax.fori_loop(0, blocks // 16, rows, 0)
+
+    def piece(side, k, part, beam, lanes):
+        return partial[side][lanes, pl.ds(((k * 2 + part) * n_beams + beam) * pitch, half), :]
+
+    for side in range(2):
+        for k in range(len(peers(side, n_low, n_high)[1])):
+
+            def encode(beam, carry):
+                for lanes in range(2):
+                    values = [piece(side, k + 1, part, beam, lanes) for part in range(2)]
+                    ceiling = jnp.max(jnp.maximum(jnp.abs(values[0]), jnp.abs(values[1])), axis=0, keepdims=True)
+                    scale[side][k, beam, lanes : lanes + 1, :] = ceiling
+                    for part in range(2):
+                        codes[side][k, beam, part, lanes] = quantize(values[part], ceiling)
+                return carry
+
+            lax.fori_loop(0, n_beams, encode, 0)
+
+    scales = {}
+    for side in range(2):
+        for k, peer in enumerate(peers(side, n_low, n_high)[1]):
+            scales[side, k] = pltpu.make_async_remote_copy(
+                src_ref=scale[side].at[k],
+                dst_ref=scale_in[side].at[k],
+                send_sem=scale_send[side].at[k],
+                recv_sem=scale_recv[side].at[k],
+                device_id=peer,
+                device_id_type=MESH,
+            )
+            scales[side, k].start()
+
+    def exchange(side, k, beam):
+        return pltpu.make_async_remote_copy(
+            src_ref=codes[side].at[k, beam],
+            dst_ref=landed[side].at[k, beam],
+            send_sem=sum_send[side].at[k, beam],
+            recv_sem=sum_recv[side].at[k, beam],
+            device_id=peers(side, n_low, n_high)[1][k],
+            device_id_type=MESH,
+        )
+
+    def each_exchange(beam, act):
+        for side in range(2):
+            for k in range(len(peers(side, n_low, n_high)[1])):
+                act(exchange(side, k, beam))
+
+    def launch(beam, carry):
+        each_exchange(beam, lambda copy: copy.start())
+        return carry
+
+    lax.fori_loop(0, n_beams, launch, 0)
+    for copy in scales.values():
+        copy.wait_recv()
+
+    def finish(beam, carry):
+        each_exchange(beam, lambda copy: copy.wait_recv())
+        for side in range(2):
+            for lanes in range(2):
+                for part in range(2):
+                    total = piece(side, 0, part, beam, lanes)
+                    for k in range(len(peers(side, n_low, n_high)[1])):
+                        ceiling = scale_in[side][k, beam, lanes : lanes + 1, :]
+                        total = total + dequantize(landed[side][k, beam, part, lanes], ceiling)
+                    out_ref[part, beam, side * half : (side + 1) * half, lanes * 128 : (lanes + 1) * 128] = total
+        return carry
+
+    lax.fori_loop(0, n_beams, finish, 0)
+
+    def drain(beam, carry):
+        each_exchange(beam, lambda copy: copy.wait_send())
+        return carry
+
+    lax.fori_loop(0, n_beams, drain, 0)
+    for copy in (*gathers.values(), *scales.values()):
+        copy.wait_send()
+
+
+def sum_beams(volts, weights, n_low, n_high, n_beams, root):
+    blocks, depth, _ = volts.shape
+    chunks = 4
+    half = root // 2
+    pitch = half + 4
+    dma = pltpu.SemaphoreType.DMA
+    groups = ((n_low, n_high), (n_high, n_low))
+    per_side = lambda make: [make(*group) for group in groups]
+    return pl.pallas_call(
+        functools.partial(beams_kernel, n_low, n_high, chunks),
+        in_specs=[pl.BlockSpec(memory_space=pltpu.VMEM)] * 3,
+        out_specs=pl.BlockSpec(memory_space=pltpu.VMEM),
+        out_shape=jax.ShapeDtypeStruct((2, n_beams, root, root), jnp.float32),
         scratch_shapes=[
-            pltpu.VMEM((rows, 2 * total_len), jnp.float32),
-            pltpu.VMEM((rows, 2048 + 128), jnp.float32),
+            *per_side(lambda g, r: pltpu.VMEM((g - 1, blocks // 2, depth, 128), jnp.bfloat16)),
+            *per_side(lambda g, r: pltpu.VMEM((2, r * 2 * n_beams * pitch, 128), jnp.float32)),
+            *per_side(lambda g, r: pltpu.VMEM((r - 1, n_beams, 2, 2, half, 128), jnp.int16)),
+            *per_side(lambda g, r: pltpu.VMEM((r - 1, n_beams, 2, 2, half, 128), jnp.int16)),
+            *per_side(lambda g, r: pltpu.VMEM((r - 1, n_beams, 8, 128), jnp.float32)),
+            *per_side(lambda g, r: pltpu.VMEM((r - 1, n_beams, 8, 128), jnp.float32)),
+            *per_side(lambda g, r: dma((g - 1, chunks))),
+            *per_side(lambda g, r: dma((g - 1, chunks))),
+            *per_side(lambda g, r: dma((r - 1, n_beams))),
+            *per_side(lambda g, r: dma((r - 1, n_beams))),
+            *per_side(lambda g, r: dma((r - 1,))),
+            *per_side(lambda g, r: dma((r - 1,))),
         ],
-    )(delays, volts)
+        compiler_params=pltpu.CompilerParams(
+            collective_id=0, has_side_effects=True, vmem_limit_bytes=60 * 1024 * 1024
+        ),
+        cost_estimate=pl.CostEstimate(
+            flops=8 * n_beams * depth * blocks * 128, bytes_accessed=2 * volts.size, transcendentals=0
+        ),
+    )(volts, *weights)
+
+
+def order_weights(own_weights, n_low, n_high, n_beams):
+    n_sta = n_low * n_high
+    w_real, w_imag = own_weights[0], own_weights[1]
+    full = jnp.stack([jnp.stack([w_real, -w_imag], axis=1), jnp.stack([w_imag, w_real], axis=1)])
+    full = full.reshape(2, n_sta, n_beams, 2, n_sta, -1)
+    sta = lax.axis_index("sta")
+    high, low = sta // n_low, lax.rem(sta, n_low)
+    in_row = lambda step, n: high * n_low + lax.rem(low + step * jnp.arange(n) + n, n)
+    in_column = lambda step, n: lax.rem(high + step * jnp.arange(n) + n, n) * n_low + low
+    out = []
+    for beam_ids, station_ids in (
+        (in_column(1, n_high), in_row(-1, n_low)),
+        (in_row(1, n_low), in_column(-1, n_high)),
+    ):
+        chosen = jnp.take(jnp.take(full, beam_ids, axis=1), station_ids, axis=4)
+        chosen = chosen.transpose(1, 0, 2, 4, 3, 5)
+        out.append(chosen.reshape(chosen.shape[0] * 2 * n_beams, -1))
+    return out
 
 
 def split(values):
@@ -178,16 +372,10 @@
     n_dev = n_sub * n_sta
     assert sub_dev == 1 and trials == 1 and root_len * root_len == total_len
     shifted = shift(voltages[0], station_delays)
-    own_weights = lax.dynamic_slice_in_dim(
-        beam_weights, lax.axis_index("sta") * local_beams, local_beams, 2
-    )[0]
-    w_real, w_imag = own_weights[0], own_weights[1]
-    volts = lax.all_gather(shifted, "sta", axis=1, tiled=True)
-    volts = volts.reshape(-1, total_len)
-    weights = jnp.concatenate(
-        [jnp.concatenate([w_real, -w_imag], axis=1), jnp.concatenate([w_imag, w_real], axis=1)], axis=0
-    )
-    beams = form_beams(weights, volts, root_len).reshape(2, local_beams, root_len, root_len)
+    n_low = 2 if n_sta % 2 == 0 else 1
+    n_high = n_sta // n_low
+    weights = order_weights(beam_weights[0], n_low, n_high, local_beams)
+    beams = sum_beams(shifted, weights, n_low, n_high, local_beams, root_len)
     subband = lax.axis_index("sub") + jnp.arange(1, dtype=jnp.int32)
     base_phase = chirp_base(subband, root_len, total_len)
     dm_value = DM_STEP * dm_index.astype(jnp.float32)

time: 348 us -> 221 us (0.64)
  waiting for transfers between devices: 149 us -> 0.01 us
  Pallas kernels: 88.4 us -> 120 us
  between operations: 14.1 us -> 0.79 us
  local copies, waits for them, and re-layouts: 2.96 us -> 6.86 us
    all_gather x1 -> x0, waiting for transfers between devices: 149 us -> none  [shards(): volts = lax.all_gather(shifted, 'sta', axis=1, tiled=True)]
    pallas_call x1, Pallas kernels: 10.8 us -> 80.4 us  [sum_beams(): pl.pallas_call(functools.partial(beams_kernel, n_low, n_high, chunks), in...]
    pallas_call x1, Pallas kernels: 50.8 us -> 13.3 us  [shift(): pl.pallas_call(shift_kernel, grid=(parts,), in_specs=[pl.BlockSpec(memory...]
  transfers between devices with their start and end apart: 2 -> 1, of which waited for: 1 -> 0; matrix products, arithmetic and copies ran while one was open for 3% -> 0% of each run, Pallas kernels for 0% -> 0%
where the time goes in v1:
time: 221 us
  Pallas kernels  120 us (54%)
  blocking collectives  69.7 us (32%)
  other arithmetic  18.4 us (8%)
  local copies, waits for them, and re-layouts  6.86 us (3%)
  starting transfers between devices  4.91 us (2%)
    pallas_call x1, Pallas kernels, sum_beams(): pl.pallas_call(functools.partial(beams_kernel, n_low, n_high, chunks), in...  80.4 us
    unnamed x1, blocking collectives  69.7 us
    pallas_call x1, Pallas kernels, dedisperse(): pl.pallas_call(dedisperse_kernel, grid=(n_beams,), in_specs=[pl.BlockSpec...  26.6 us
    pallas_call x1, Pallas kernels, shift(): pl.pallas_call(shift_kernel, grid=(parts,), in_specs=[pl.BlockSpec(memory...  13.3 us
    sin x1, other arithmetic, shards(): sent = dedisperse(beams, jnp.cos(phase_table), jnp.sin(phase_table), n_dev)  8.82 us
    all_to_all x1, starting transfers between devices, shards(): lax.all_to_all(sent, ('sub', 'sta'), split_axis=0, concat_axis=0, tiled=T...  4.91 us
  transfers between devices with their start and end apart: 1, of which 0 were waited for; matrix products, arithmetic and copies ran while one was open for 0% of the time, Pallas kernels for 0%

profile of v1, /device:TPU:0, one launch (start us, length us, event | category | flops | bytes accessed | tf_op | source)
XLA Modules:
  0.0 220.9 jit_solution(9410492654626492558)
XLA Ops:
  0.7 0.7 fusion.13
  1.4 0.1 squeeze.5
  1.5 0.1 stack.14
  1.7 0.6 gather_fusion
  2.3 0.1 select_bitcast_fusion.1
  2.4 0.6 gather_fusion.1
  2.9 0.1 select_bitcast_fusion.3
  3.0 0.7 reshape.165.w0_ref
  3.7 0.6 gather_fusion.2
  4.3 0.1 select_bitcast_fusion
  4.4 0.6 gather_fusion.3
  5.0 0.1 select_bitcast_fusion.2
  5.1 0.7 reshape.166.w1_ref
  5.8 0.7 multiply_bitcast_fusion
  6.4 13.3 %shard_map.86.volt_ref = bf16[512,32,128]{2,1,0:T(8,128)(2,1)} custom-call(s32[16]{0:T(128)} %delay_ref.1, bf16[2,16,65536]{2,1,0:T(8,128)(2,1)} %bitcast.29), custom_call_target="tpu_custom_call" | custom-call | tf_op jit(solution)/shard_map/pallas_call | solution.py:82
  19.7 80.4 %shard_map.87.x_ref = f32[2,8,256,256]{3,2,1,0:T(8,128)} custom-call(bf16[512,32,128]{2,1,0:T(8,128)(2,1)} %shard_map.86.volt_ref, bf16[32,64]{1,0:T(8,128)(2,1)} %reshape.165.w0_ref, bf16[32,64]{1,0:T(8,128)(2,1)} %reshape.166.w1_ref), custom_call_target="tpu_custom_call" | custom-call | flops 134217728 | bytes 4194304 | tf_op jit(solution)/shard_map/pallas_call | solution.py:254
  100.1 2.6 %add_reduce_fusion = f32[8]{0:T(128)S(1)} fusion(f32[2,8,256,256]{3,2,1,0:T(8,128)} %shard_map.87.x_ref), kind=kLoop, calls=%fused_computation.12 | loop fusion | flops 2097144 | bytes 4194336 | tf_op jit(solution)/shard_map/reduce_sum | solution.py:384
  102.7 0.1 multiply_divide_fusion
  102.8 8.8 %multiply_sine_fusion = (f32[8,256,256]{2,1,0:T(8,128)}, f32[8,256,256]{2,1,0:T(8,128)}) fusion(f32[256,256]{1,0:T(8,128)S(1)} %multiply_divide_fusion, f32[8]{0:T(128)S(1)} %multiply_bitcast_fusion), kind=kLoop, calls=%fused_computation.6 | loop fusion | flops 524288 | bytes 4456480 | tf_op jit(solution)/shard_map/sin | solution.py:383
  111.6 0.1 multiply_dynamic-update-slice_fusion
  111.7 26.6 %shard_map.88 = f32[32,2,8,16,128]{4,3,2,1,0:T(8,128)} custom-call(f32[2,8,256,256]{3,2,1,0:T(8,128)} %shard_map.87.x_ref, f32[8,256,256]{2,1,0:T(8,128)} %get-tuple-element.19.h_real_ref, f32[8,256,256]{2,1,0:T(8,128)} %get-tuple-element.18.h_imag_ref, bf16[2,512,512]{2,1,0:T(8,128)(2,1)} %constant.101.clone.left_ref, ...), custom_call_target="tpu_custom_call" | custom-call | flops 12884901888 | bytes 12582912 | tf_op jit(solution)/shard_map/pallas_call | solution.py:344
  138.4 4.2 %multiply_convert_fusion = f16[32,2,8,16,128]{4,3,2,1,0:T(8,128)(2,1)} fusion(f32[32,2,8,16,128]{4,3,2,1,0:T(8,128)} %shard_map.88, f32[8]{0:T(128)S(1)} %get-tuple-element.25), kind=kLoop, calls=%fused_computation.5 | loop fusion | flops 2097152 | bytes 6291488 | tf_op jit(solution)/shard_map/convert_element_type | solution.py:388
  142.6 4.9 %all-to-all-start = ((f16[32,2,8,16,128]{4,3,2,1,0:T(8,128)(2,1)}), f16[32,2,8,16,128]{4,3,2,1,0:T(8,128)(2,1)S(1)}, u32[]{:S(2)}, u32[]{:S(2)}) async-start(f16[32,2,8,16,128]{4,3,2,1,0:T(8,128)(2,1)} %multiply_convert_fusion), calls=%async_computation | async-start | bytes 4194304 | tf_op jit(solution)/shard_map/all_to_all | solution.py:389
  147.5 69.7 %all-reduce = f32[256]{0:T(256)S(1)} all-reduce(f32[256]{0:T(256)S(1)} %get-tuple-element.24), channel_id=2, replica_groups=mesh['sub'=8,'sta'=4] {'sub','sta'}, use_global_device_ids=true, to_apply=%add | all-reduce | flops 256 | bytes 2048
  217.2 0.1 reshape.203
  217.3 0.0 all-to-all-done
  217.3 0.4 convert_multiply_fusion
  217.7 0.5 copy.28
  218.2 0.0 copy-start
  218.2 0.3 fusion.1
  218.5 1.7 copy-done
  220.2 0.7 broadcast_multiply_fusion
  (15 shorter events, 0.2 us)
Async XLA Ops:
  142.6 74.7 %all-to-all-start = ((f16[32,2,8,16,128]{4,3,2,1,0:T(8,128)(2,1)}), f16[32,2,8,16,128]{4,3,2,1,0:T(8,128)(2,1)S(1)}, u32[]{:S(2)}, u32[]{:S(2)}) async-start(f16[32,2,8,16,128]{4,3,2,1,0:T(8,128)(2,1)} %multiply_convert_fusion), calls=%async_computation | async-start | bytes 4194304 | tf_op jit(solution)/shard_map/all_to_all | solution.py:389
  218.2 2.0 copy-start

commit v2 on v1

--- a/solution.py
+++ b/solution.py
@@ -89,6 +89,16 @@
     )(delays, volts)
 
 
+def split(values):
+    high = values.astype(jnp.bfloat16)
+    return high, (values - high.astype(jnp.float32)).astype(jnp.bfloat16)
+
+
+def dot3(a_high, a_low, b_high, b_low):
+    dot = functools.partial(jnp.dot, preferred_element_type=jnp.float32)
+    return dot(a_high, b_high) + (dot(a_high, b_low) + dot(a_low, b_high))
+
+
 MESH = pl.DeviceIdType.MESH
 PEAK = 32767.0
 
@@ -111,21 +121,83 @@
     return codes.astype(jnp.int32).astype(jnp.float32) * (ceiling * (1.0 / PEAK))
 
 
-def beams_kernel(n_low, n_high, chunks, volt_ref, w0_ref, w1_ref, out_ref, *scratch):
+def turn(phase):
+    count = jnp.round(phase * 0.6366197723675814)
+    rest = ((phase - count * 1.5703125) - count * 4.837512969970703125e-4) - count * 7.54978995489188216e-8
+    square = rest * rest
+    sine = rest + rest * square * (
+        (-1.9515295891e-4 * square + 8.3321608736e-3) * square - 1.6666654611e-1
+    )
+    cosine = (1.0 - 0.5 * square) + square * square * (
+        (2.443315711809948e-5 * square - 1.388731625493765e-3) * square + 4.166664568298827e-2
+    )
+    quarter = count.astype(jnp.int32)
+    odd = (quarter & 1) == 1
+    real, imag = jnp.where(odd, sine, cosine), jnp.where(odd, cosine, sine)
+    real = jnp.where(((quarter + 1) & 2) == 2, -real, real)
+    imag = jnp.where((quarter & 2) == 2, -imag, imag)
+    return real, imag
+
+
+def disperse(x, h_real, h_imag, left_ref, right_ref, twist_ref):
+    root = twist_ref.shape[1]
+    cos_twist, sin_twist = twist_ref[0], twist_ref[1]
+    a = dot3(left_ref[0], left_ref[1], *split(x))
+    a_real, a_imag = a[:root], a[root:]
+    b = jnp.concatenate(
+        [a_real * cos_twist + a_imag * sin_twist, a_imag * cos_twist - a_real * sin_twist], axis=1
+    )
+    s = dot3(*split(b), right_ref[0], right_ref[1])
+    s_real, s_imag = s[:, :root], s[:, root:]
+    c = jnp.concatenate([s_real * h_real - s_imag * h_imag, s_real * h_imag + s_imag * h_real], axis=1)
+    d = dot3(*split(c), left_ref[0], left_ref[1])
+    d_real, d_imag = d[:, :root], d[:, root:]
+    e = jnp.concatenate(
+        [d_real * cos_twist - d_imag * sin_twist, d_imag * cos_twist + d_real * sin_twist], axis=0
+    )
+    return dot3(right_ref[0], right_ref[1], *split(e)) * (1.0 / (root * root))
+
+
+def series_kernel(
+    n_low,
+    n_high,
+    chunks,
+    dm_ref,
+    volt_ref,
+    w0_ref,
+    w1_ref,
+    base_ref,
+    left_ref,
+    right_ref,
+    twist_ref,
+    out_ref,
+    peak_ref,
+    *scratch,
+):
     got, partial, codes, landed, scale, scale_in = (scratch[2 * i : 2 * i + 2] for i in range(6))
     gather_send, gather_recv, sum_send, sum_recv, scale_send, scale_recv = (
         scratch[12 + 2 * i : 14 + 2 * i] for i in range(6)
     )
+    chirp, flat, ready, ready_peak, middle, middle_peak = scratch[24:30]
+    move_send, move_recv, peak_send, peak_recv, pass_send, pass_recv, last_send, last_recv, own_sem = scratch[30:]
     weight_refs = (w0_ref, w1_ref)
-    n_beams, root = out_ref.shape[1:3]
+    n_sta, n_beams, n_sub, _, rows_out, _ = out_ref.shape
+    root = twist_ref.shape[1]
+    n_dev = n_sub * n_sta
+    sub, sta = lax.axis_index("sub"), lax.axis_index("sta")
+    sub_peer = lambda k: lax.rem(sub + k, n_sub)
+    sta_peer = lambda k: lax.rem(sta + k, n_sta)
     half = root // 2
     pitch = partial[0].shape[1] // weight_refs[0].shape[0]
     blocks = volt_ref.shape[0] // 2 // chunks
 
     barrier = pltpu.get_barrier_semaphore()
-    for peer in (*peers(0, n_low, n_high)[0], *peers(0, n_low, n_high)[1]):
-        pl.semaphore_signal(barrier, inc=1, device_id=peer, device_id_type=MESH)
-    pl.semaphore_wait(barrier, n_low + n_high - 2)
+
+    for k in range(1, n_sub):
+        pl.semaphore_signal(barrier, inc=1, device_id=(sub_peer(k), sta), device_id_type=MESH)
+    for k in range(1, n_sta):
+        pl.semaphore_signal(barrier, inc=1, device_id=(sub, sta_peer(k)), device_id_type=MESH)
+    pl.semaphore_wait(barrier, n_sub + n_sta - 2)
 
     gathers = {}
     for chunk in range(chunks):
@@ -141,6 +213,16 @@
                 )
                 copy.start()
                 gathers[side, k, chunk] = copy
+
+    def turns(beam, carry):
+        measure = DM_STEP * dm_ref[beam, 0].astype(jnp.float32)
+        for part in range(0, root, 64):
+            chirp[beam, 0, part : part + 64], chirp[beam, 1, part : part + 64] = turn(
+                measure * base_ref[0, part : part + 64]
+            )
+        return carry
+
+    lax.fori_loop(0, n_beams, turns, 0)
 
     for chunk in range(chunks):
         for side in range(2):
@@ -220,19 +302,99 @@
     for copy in scales.values():
         copy.wait_recv()
 
+    def move(beam, k):
+        return pltpu.make_async_remote_copy(
+            src_ref=ready.at[sub_peer(k), beam],
+            dst_ref=middle.at[beam, sub],
+            send_sem=move_send.at[beam, k - 1],
+            recv_sem=move_recv.at[beam, k - 1],
+            device_id=(sub_peer(k), sta),
+            device_id_type=MESH,
+        )
+
+    def move_peak(k):
+        return pltpu.make_async_remote_copy(
+            src_ref=ready_peak,
+            dst_ref=middle_peak.at[sub],
+            send_sem=peak_send.at[k - 1],
+            recv_sem=peak_recv.at[k - 1],
+            device_id=(sub_peer(k), sta),
+            device_id_type=MESH,
+        )
+
+    def forward(beam, k):
+        return pltpu.make_async_remote_copy(
+            src_ref=middle.at[beam, :, sta_peer(k)],
+            dst_ref=out_ref.at[sta, beam],
+            send_sem=pass_send.at[beam, k - 1],
+            recv_sem=pass_recv.at[beam, k - 1],
+            device_id=(sub, sta_peer(k)),
+            device_id_type=MESH,
+        )
+
+    def forward_peak(k):
+        return pltpu.make_async_remote_copy(
+            src_ref=middle_peak,
+            dst_ref=peak_ref.at[sta],
+            send_sem=last_send.at[k - 1],
+            recv_sem=last_recv.at[k - 1],
+            device_id=(sub, sta_peer(k)),
+            device_id_type=MESH,
+        )
+
+    def keep(beam):
+        return pltpu.make_async_copy(middle.at[beam, :, sta], out_ref.at[sta, beam], own_sem.at[beam])
+
     def finish(beam, carry):
         each_exchange(beam, lambda copy: copy.wait_recv())
-        for side in range(2):
-            for lanes in range(2):
-                for part in range(2):
+        quarters = []
+        for part in range(2):
+            for side in range(2):
+                pair = []
+                for lanes in range(2):
                     total = piece(side, 0, part, beam, lanes)
                     for k in range(len(peers(side, n_low, n_high)[1])):
                         ceiling = scale_in[side][k, beam, lanes : lanes + 1, :]
                         total = total + dequantize(landed[side][k, beam, part, lanes], ceiling)
-                    out_ref[part, beam, side * half : (side + 1) * half, lanes * 128 : (lanes + 1) * 128] = total
+                    pair.append(total)
+                quarters.append(jnp.concatenate(pair, axis=1))
+        x = jnp.concatenate(quarters, axis=0)
+        series = disperse(x, chirp[beam, 0], chirp[beam, 1], left_ref, right_ref, twist_ref)
+        for part in range(2):
+            for lanes in range(2):
+                flat[part, pl.ds(lanes, root, 2), :] = series[
+                    part * root : (part + 1) * root, lanes * half : (lanes + 1) * half
+                ]
+        values = [flat[part] for part in range(2)]
+        ceiling = jnp.max(jnp.maximum(jnp.abs(values[0]), jnp.abs(values[1])), axis=0, keepdims=True)
+        ready_peak[pl.ds(beam, 1), :] = ceiling
+        for part in range(2):
+            ready[:, beam, :, part] = quantize(values[part], ceiling).reshape(n_sub, n_sta, rows_out, half)
+        middle[beam, sub] = ready[sub, beam]
+        for k in range(1, n_sub):
+            move(beam, k).start()
         return carry
 
     lax.fori_loop(0, n_beams, finish, 0)
+    middle_peak[sub] = ready_peak[...]
+    for k in range(1, n_sub):
+        move_peak(k).start()
+
+    def spread(beam, carry):
+        for k in range(1, n_sub):
+            move(beam, k).wait_recv()
+        for k in range(1, n_sta):
+            forward(beam, k).start()
+        keep(beam).start()
+        return carry
+
+    lax.fori_loop(0, n_beams, spread, 0)
+    for k in range(1, n_sub):
+        move_peak(k).wait_recv()
+    for k in range(1, n_sta):
+        forward_peak(k).start()
+    own_peak = pltpu.make_async_copy(middle_peak, peak_ref.at[sta], own_sem.at[n_beams])
+    own_peak.start()
 
     def drain(beam, carry):
         each_exchange(beam, lambda copy: copy.wait_send())
@@ -241,21 +403,45 @@
     lax.fori_loop(0, n_beams, drain, 0)
     for copy in (*gathers.values(), *scales.values()):
         copy.wait_send()
-
-
-def sum_beams(volts, weights, n_low, n_high, n_beams, root):
+    own_peak.wait()
+    for k in range(1, n_sub):
+        move_peak(k).wait_send()
+    for k in range(1, n_sta):
+        forward_peak(k).wait()
+
+    def settle(beam, carry):
+        keep(beam).wait()
+        for k in range(1, n_sub):
+            move(beam, k).wait_send()
+        for k in range(1, n_sta):
+            forward(beam, k).wait()
+        return carry
+
+    lax.fori_loop(0, n_beams, settle, 0)
+
+
+def make_series(dm_index, volts, weights, base_phase, n_low, n_high, n_sub, root):
     blocks, depth, _ = volts.shape
     chunks = 4
+    n_beams = dm_index.shape[0]
     half = root // 2
+    n_sta = n_low * n_high
+    rows_out = 2 * root // (n_sub * n_sta)
+    tables = dft_tables(root)
+    vmem = pl.BlockSpec(memory_space=pltpu.VMEM)
+    hbm = pl.BlockSpec(memory_space=pltpu.HBM)
     pitch = half + 4
     dma = pltpu.SemaphoreType.DMA
     groups = ((n_low, n_high), (n_high, n_low))
     per_side = lambda make: [make(*group) for group in groups]
     return pl.pallas_call(
-        functools.partial(beams_kernel, n_low, n_high, chunks),
-        in_specs=[pl.BlockSpec(memory_space=pltpu.VMEM)] * 3,
-        out_specs=pl.BlockSpec(memory_space=pltpu.VMEM),
-        out_shape=jax.ShapeDtypeStruct((2, n_beams, root, root), jnp.float32),
+        functools.partial(series_kernel, n_low, n_high, chunks),
+        in_specs=[pl.BlockSpec(memory_space=pltpu.SMEM), *[vmem] * 7],
+        out_specs=(hbm, hbm),
+        out_shape=(
+            jax.ShapeDtypeStruct((n_sta, n_beams, n_sub, 2, rows_out, 128), jnp.int16),
+            jax.ShapeDtypeStruct((n_sta, n_sub, n_beams, 128), jnp.float32),
+        ),
         scratch_shapes=[
             *per_side(lambda g, r: pltpu.VMEM((g - 1, blocks // 2, depth, 128), jnp.bfloat16)),
             *per_side(lambda g, r: pltpu.VMEM((2, r * 2 * n_beams * pitch, 128), jnp.float32)),
@@ -269,6 +455,21 @@
             *per_side(lambda g, r: dma((r - 1, n_beams))),
             *per_side(lambda g, r: dma((r - 1,))),
             *per_side(lambda g, r: dma((r - 1,))),
+            pltpu.VMEM((n_beams, 2, root, root), jnp.float32),
+            pltpu.VMEM((2, 2 * root, 128), jnp.float32),
+            pltpu.VMEM((n_sub, n_beams, n_sta, 2, rows_out, 128), jnp.int16),
+            pltpu.VMEM((n_beams, 128), jnp.float32),
+            pltpu.VMEM((n_beams, n_sub, n_sta, 2, rows_out, 128), jnp.int16),
+            pltpu.VMEM((n_sub, n_beams, 128), jnp.float32),
+            dma((n_beams, n_sub - 1)),
+            dma((n_beams, n_sub - 1)),
+            dma((n_sub - 1,)),
+            dma((n_sub - 1,)),
+            dma((n_beams, n_sta - 1)),
+            dma((n_beams, n_sta - 1)),
+            dma((n_sta - 1,)),
+            dma((n_sta - 1,)),
+            dma((n_beams + 1,)),
         ],
         compiler_params=pltpu.CompilerParams(
             collective_id=0, has_side_effects=True, vmem_limit_bytes=60 * 1024 * 1024
@@ -276,7 +477,7 @@
         cost_estimate=pl.CostEstimate(
             flops=8 * n_beams * depth * blocks * 128, bytes_accessed=2 * volts.size, transcendentals=0
         ),
-    )(volts, *weights)
+    )(dm_index, volts, *weights, base_phase, *tables)
 
 
 def order_weights(own_weights, n_low, n_high, n_beams):
@@ -299,68 +500,6 @@
     return out
 
 
-def split(values):
-    high = values.astype(jnp.bfloat16)
-    return high, (values - high.astype(jnp.float32)).astype(jnp.bfloat16)
-
-
-def dot3(a_high, a_low, b_high, b_low):
-    dot = functools.partial(jnp.dot, preferred_element_type=jnp.float32)
-    return dot(a_high, b_high) + (dot(a_high, b_low) + dot(a_low, b_high))
-
-
-def dedisperse_kernel(x_ref, h_real_ref, h_imag_ref, left_ref, right_ref, twist_ref, out_ref, flat):
-    root = twist_ref.shape[1]
-    half = root // 2
-    cos_twist, sin_twist = twist_ref[0], twist_ref[1]
-    x = x_ref[...].reshape(2 * root, root)
-    a = dot3(left_ref[0], left_ref[1], *split(x))
-    a_real, a_imag = a[:root], a[root:]
-    b = jnp.concatenate(
-        [a_real * cos_twist + a_imag * sin_twist, a_imag * cos_twist - a_real * sin_twist], axis=1
-    )
-    s = dot3(*split(b), right_ref[0], right_ref[1])
-    s_real, s_imag = s[:, :root], s[:, root:]
-    h_real, h_imag = h_real_ref[0], h_imag_ref[0]
-    c = jnp.concatenate([s_real * h_real - s_imag * h_imag, s_real * h_imag + s_imag * h_real], axis=1)
-    d = dot3(*split(c), left_ref[0], left_ref[1])
-    d_real, d_imag = d[:, :root], d[:, root:]
-    e = jnp.concatenate(
-        [d_real * cos_twist - d_imag * sin_twist, d_imag * cos_twist + d_real * sin_twist], axis=0
-    )
-    out = dot3(right_ref[0], right_ref[1], *split(e)) * (1.0 / (root * root))
-    for part in range(2):
-        for side in range(2):
-            flat[pl.ds(side, root, 2), :] = out[part * root : (part + 1) * root, side * half : (side + 1) * half]
-        out_ref[:, part, 0] = flat[...].reshape(out_ref.shape[0], out_ref.shape[3], half)
-
-
-def dedisperse(beams, h_real, h_imag, n_dev):
-    _, n_beams, root, _ = beams.shape
-    left, right, twist = dft_tables(root)
-    rows = 2 * root // n_dev
-    whole = lambda shape: pl.BlockSpec(shape, lambda b: (0,) * len(shape))
-    own = pl.BlockSpec((1, root, root), lambda b: (b, 0, 0))
-    return pl.pallas_call(
-        dedisperse_kernel,
-        grid=(n_beams,),
-        in_specs=[
-            pl.BlockSpec((2, 1, root, root), lambda b: (0, b, 0, 0)),
-            own,
-            own,
-            whole(left.shape),
-            whole(right.shape),
-            whole(twist.shape),
-        ],
-        out_specs=pl.BlockSpec((n_dev, 2, 1, rows, root // 2), lambda b: (0, 0, b, 0, 0)),
-        out_shape=jax.ShapeDtypeStruct((n_dev, 2, n_beams, rows, root // 2), jnp.float32),
-        scratch_shapes=[pltpu.VMEM((2 * root, root // 2), jnp.float32)],
-        cost_estimate=pl.CostEstimate(
-            flops=96 * n_beams * root**3, bytes_accessed=24 * n_beams * root**2, transcendentals=0
-        ),
-    )(beams, h_real, h_imag, left, right, twist)
-
-
 def shards(voltages, beam_weights, station_delays, dm_index):
     sub_dev = voltages.shape[0]
     total_len = voltages.shape[3]
@@ -369,26 +508,16 @@
     root_len = int(round(total_len**0.5))
     n_sub = lax.axis_size("sub")
     n_sta = lax.axis_size("sta")
-    n_dev = n_sub * n_sta
     assert sub_dev == 1 and trials == 1 and root_len * root_len == total_len
-    shifted = shift(voltages[0], station_delays)
     n_low = 2 if n_sta % 2 == 0 else 1
     n_high = n_sta // n_low
+    shifted = shift(voltages[0], station_delays)
     weights = order_weights(beam_weights[0], n_low, n_high, local_beams)
-    beams = sum_beams(shifted, weights, n_low, n_high, local_beams, root_len)
     subband = lax.axis_index("sub") + jnp.arange(1, dtype=jnp.int32)
     base_phase = chirp_base(subband, root_len, total_len)
-    dm_value = DM_STEP * dm_index.astype(jnp.float32)
-    phase_table = dm_value[:, :, None] * base_phase
-    sent = dedisperse(beams, jnp.cos(phase_table), jnp.sin(phase_table), n_dev)
-    power = jnp.mean(beams[0] * beams[0] + beams[1] * beams[1], axis=(1, 2))
-    rms = jnp.where(power > 0, jnp.sqrt(power), 1.0)
-    gain = 32768.0 / root_len / rms
-    undo = lax.all_gather(rms * (root_len / 32768.0), ("sub", "sta"), axis=0)
-    sent = (sent * gain[None, None, :, None, None]).astype(jnp.float16)
-    moved = lax.all_to_all(sent, ("sub", "sta"), split_axis=0, concat_axis=0, tiled=True)
-    moved = moved.astype(jnp.float32) * undo[:, None, :, None, None]
-    moved = moved.reshape(n_sub, n_sta, *moved.shape[1:]).transpose(0, 2, 1, 3, 4, 5)
+    codes, peak = make_series(dm_index, shifted, weights, base_phase, n_low, n_high, n_sub, root_len)
+    peak = peak.transpose(1, 0, 2, 3)[:, None, :, :, None, :]
+    moved = dequantize(codes.transpose(2, 3, 0, 1, 4, 5), peak)
     moved = moved.reshape(n_sub, 2, n_sta * local_beams, *moved.shape[4:])
     intensity = jnp.mean(moved[:, 0] * moved[:, 0] + moved[:, 1] * moved[:, 1], axis=0)
     return (moved.reshape(*moved.shape[:3], 1, -1), intensity.reshape(intensity.shape[0], 1, -1))

time: 221 us -> 149 us (0.67)
  blocking collectives: 69.7 us -> 0 us
  Pallas kernels: 120 us -> 134 us
  other arithmetic: 18.4 us -> 5.53 us
  starting transfers between devices: 4.91 us -> 0 us
    unnamed x1 -> x0, blocking collectives: 69.7 us -> none
    pallas_call x2 -> x1, Pallas kernels: 107 us -> 120 us  [make_series(): pl.pallas_call(functools.partial(series_kernel, n_low, n_high, chunks), i...]
    sin x1 -> x0, other arithmetic: 8.82 us -> none  [shards(): sent = dedisperse(beams, jnp.cos(phase_table), jnp.sin(phase_table), n_dev)]
    all_to_all x1 -> x0, starting transfers between devices: 4.91 us -> none  [shards(): lax.all_to_all(sent, ('sub', 'sta'), split_axis=0, concat_axis=0, tiled=T...]
    convert_element_type x1 -> x0, other arithmetic: 4.22 us -> none  [shards(): sent = (sent * gain[None, None, :, None, None]).astype(jnp.float16)]
    reduce_sum x1 -> x0, other arithmetic: 2.62 us -> none  [shards(): power = jnp.mean(beams[0] * beams[0] + beams[1] * beams[1], axis=(1, 2))]
    unnamed x3 -> x2, local copies, waits for them, and re-layouts: 1.7 us -> 3.95 us
  transfers between devices with their start and end apart: 1 -> 0, of which waited for: 0 -> 0; matrix products, arithmetic and copies ran while one was open for 0% -> 0% of each run, Pallas kernels for 0% -> 0%
where the time goes in v2:
time: 149 us; the launch traced here: 148 us
  Pallas kernels  134 us (90%)
  local copies, waits for them, and re-layouts  8.56 us (6%)
  other arithmetic  5.53 us (4%)
    pallas_call x1, Pallas kernels, make_series(): pl.pallas_call(functools.partial(series_kernel, n_low, n_high, chunks), i...  120 us
    pallas_call x1, Pallas kernels, shift(): pl.pallas_call(shift_kernel, grid=(parts,), in_specs=[pl.BlockSpec(memory...  13.3 us
    unnamed x2, local copies, waits for them, and re-layouts  3.95 us

profile of v2, /device:TPU:0, one launch (start us, length us, event | category | flops | bytes accessed | tf_op | source)
XLA Modules:
  0.0 148.4 jit_solution(7724720043732428985)
XLA Ops:
  0.8 1.3 copy.32.dm_ref
  2.1 0.7 fusion.13
  2.8 0.1 squeeze.5
  2.9 0.1 stack.14
  3.1 0.6 gather_fusion.2
  3.6 0.6 gather_fusion
  4.2 0.1 select_bitcast_fusion.1
  4.3 0.1 select_bitcast_fusion
  4.4 0.6 gather_fusion.3
  4.9 0.1 select_bitcast_fusion.2
  5.0 0.7 reshape.155.w1_ref
  5.7 0.6 gather_fusion.1
  6.3 0.1 select_bitcast_fusion.3
  6.4 0.7 reshape.154.w0_ref
  7.1 0.8 multiply_divide_fusion.base_ref
  7.9 13.3 %shard_map.86.volt_ref = bf16[512,32,128]{2,1,0:T(8,128)(2,1)} custom-call(s32[16]{0:T(128)} %delay_ref.1, bf16[2,16,65536]{2,1,0:T(8,128)(2,1)} %bitcast.25), custom_call_target="tpu_custom_call" | custom-call | tf_op jit(solution)/shard_map/pallas_call | solution.py:82
  21.2 120.3 %shard_map.87 = (s16[4,8,8,2,16,128]{5,4,3,2,1,0:T(8,128)(2,1)}, f32[4,8,8,128]{3,2,1,0:T(8,128)}) custom-call(s32[8,1]{1,0:T(8,128)} %copy.32.dm_ref, bf16[512,32,128]{2,1,0:T(8,128)(2,1)} %shard_map.86.volt_ref, bf16[32,64]{1,0:T(8,128)(2,1)} %reshape.154.w0_ref, bf16[32,64]{1,0:T(8,128)(2,1)} %reshape.155.w1_ref, ...), custom_call_target="tpu_custom_call" | custom-call | flops 134217728 | bytes 4194304 | tf_op jit(solution)/shard_map/pallas_call | solution.py:437
  141.5 0.9 multiply_bitcast_fusion
  142.4 2.4 %bitcast_multiply_fusion = f32[8,2,4,8,16,128]{5,4,1,0,3,2:T(8,128)S(1)} fusion(s16[4,8,8,2,16,128]{5,4,3,2,1,0:T(8,128)(2,1)} %get-tuple-element.6, f32[8,4,8,128]{3,0,2,1:T(8,128)S(1)} %copy.33), kind=kLoop, calls=%fused_computation.4 | loop fusion | flops 3145728 | bytes 6422528 | tf_op jit(solution)/shard_map/mul | solution.py:121
  144.8 0.3 fusion.1
  145.1 0.7 broadcast_multiply_fusion
  145.8 2.6 %copy.35 = f32[8,2,4,8,16,128]{5,4,3,2,1,0:T(8,128)} copy(f32[8,2,4,8,16,128]{5,4,1,0,3,2:T(8,128)S(1)} %bitcast_multiply_fusion) | data formatting | bytes 8388608
  (15 shorter events, 0.2 us)

commit v3 on v2

--- a/solution.py
+++ b/solution.py
@@ -39,56 +39,6 @@
     return TWO_PI * DISPERSION * offset * offset / (centre * centre * (centre + offset))
 
 
-def shift_kernel(delay_ref, x_ref, out_ref, source, moved):
-    rows, total_len = x_ref.shape[1:]
-    blocks = total_len // 128
-    pitch = source.shape[0] // (blocks + 16)
-    def load(i, carry):
-        for u in range(8):
-            j = i * 8 + u
-            source[pl.ds(j*pitch, rows), :] = x_ref[0, :, pl.ds(pl.multiple_of(j * 128, 128), 128)].astype(jnp.float32)
-        return carry
-    lax.fori_loop(0, blocks // 8, load, 0)
-    for u in range(16):
-        source[pl.ds((blocks + u) * pitch, rows), :] = source[pl.ds(u * pitch, rows), :]
-    lane = lax.broadcasted_iota(jnp.int32, (8, 128), 1)
-    for row in range(rows):
-        delay = delay_ref[row]
-        fine = delay & 127
-        coarse = delay >> 7
-        keep = lane < 128 - fine
-        def chunk(i, carry):
-            for u in range(32):
-                j = i * (8*32) + u * 8
-                start = (j - coarse - 1) & (blocks - 1)
-                before = source[pl.ds(start * pitch + row, 8, stride=pitch), :]
-                after = source[pl.ds((start + 1) * pitch + row, 8, stride=pitch), :]
-                values = pltpu.roll(jnp.where(keep, after, before), fine, 1)
-                moved[pl.ds(j * pitch + row, 8, stride=pitch), :] = values
-            return carry
-        lax.fori_loop(0, blocks // (8*32), chunk, 0)
-    def store(i, carry):
-        for u in range(8):
-            j = i * 8 + u
-            out_ref[j] = moved[pl.ds(j*pitch, rows), :].astype(out_ref.dtype)
-        return carry
-    lax.fori_loop(0, blocks // 8, store, 0)
-
-
-def shift(volts, delays):
-    parts, rows, total_len = volts.shape
-    blocks = total_len // 128
-    pitch = rows + 4
-    return pl.pallas_call(
-        shift_kernel,
-        grid=(parts,),
-        in_specs=[pl.BlockSpec(memory_space=pltpu.SMEM), pl.BlockSpec((1, rows, total_len), lambda i: (i, 0, 0))],
-        out_specs=pl.BlockSpec((blocks, rows, 128), lambda i: (0, i, 0)),
-        out_shape=jax.ShapeDtypeStruct((blocks, parts * rows, 128), volts.dtype),
-        scratch_shapes=[pltpu.VMEM(((blocks + 16) * pitch, 128), jnp.float32), pltpu.VMEM((blocks * pitch, 128), jnp.float32)],
-    )(delays, volts)
-
-
 def split(values):
     high = values.astype(jnp.bfloat16)
     return high, (values - high.astype(jnp.float32)).astype(jnp.bfloat16)
@@ -163,9 +113,9 @@
     n_high,
     chunks,
     dm_ref,
-    volt_ref,
-    w0_ref,
-    w1_ref,
+    delay_ref,
+    raw_ref,
+    weight_ref,
     base_ref,
     left_ref,
     right_ref,
@@ -179,8 +129,8 @@
         scratch[12 + 2 * i : 14 + 2 * i] for i in range(6)
     )
     chirp, flat, ready, ready_peak, middle, middle_peak = scratch[24:30]
-    move_send, move_recv, peak_send, peak_recv, pass_send, pass_recv, last_send, last_recv, own_sem = scratch[30:]
-    weight_refs = (w0_ref, w1_ref)
+    weight_refs, volt_ref, source, moved, signed = scratch[39:41], *scratch[41:]
+    move_send, move_recv, peak_send, peak_recv, pass_send, pass_recv, last_send, last_recv, own_sem = scratch[30:39]
     n_sta, n_beams, n_sub, _, rows_out, _ = out_ref.shape
     root = twist_ref.shape[1]
     n_dev = n_sub * n_sta
@@ -199,23 +149,101 @@
         pl.semaphore_signal(barrier, inc=1, device_id=(sub, sta_peer(k)), device_id_type=MESH)
     pl.semaphore_wait(barrier, n_sub + n_sta - 2)
 
-    gathers = {}
-    for chunk in range(chunks):
+    stations, total_len = raw_ref.shape[1:]
+    depth = 2 * stations
+    spread_rows = depth + 4
+    all_blocks = total_len // 128
+
+    def unpack(i, carry):
+        for u in range(8):
+            block = i * 8 + u
+            for part in range(2):
+                source[pl.ds(block * spread_rows + part * stations, stations), :] = raw_ref[
+                    part, :, pl.ds(pl.multiple_of(block * 128, 128), 128)
+                ].astype(jnp.float32)
+        return carry
+
+    lax.fori_loop(0, all_blocks // 8, unpack, 0)
+    for block in range(16):
+        source[pl.ds((all_blocks + block) * spread_rows, depth), :] = source[
+            pl.ds(block * spread_rows, depth), :
+        ]
+    lane = lax.broadcasted_iota(jnp.int32, (8, 128), 1)
+
+    def gather(side, k, chunk):
+        return pltpu.make_async_remote_copy(
+            src_ref=volt_ref.at[pl.ds((side * chunks + chunk) * blocks, blocks)],
+            dst_ref=got[side].at[k, pl.ds(chunk * blocks, blocks)],
+            send_sem=gather_send[side].at[k, chunk],
+            recv_sem=gather_recv[side].at[k, chunk],
+            device_id=peers(side, n_low, n_high)[0][k],
+            device_id_type=MESH,
+        )
+
+    def shift_chunk(chunk, carry):
         for side in range(2):
-            for k, peer in enumerate(peers(side, n_low, n_high)[0]):
-                copy = pltpu.make_async_remote_copy(
-                    src_ref=volt_ref.at[pl.ds((side * chunks + chunk) * blocks, blocks)],
-                    dst_ref=got[side].at[k, pl.ds(chunk * blocks, blocks)],
-                    send_sem=gather_send[side].at[k, chunk],
-                    recv_sem=gather_recv[side].at[k, chunk],
-                    device_id=peer,
-                    device_id_type=MESH,
-                )
-                copy.start()
-                gathers[side, k, chunk] = copy
+            first = (side * chunks + chunk) * blocks
+
+            def shift_rows(i, carry):
+                for u in range(4):
+                    row = i * 4 + u
+                    delay = delay_ref[row & (stations - 1)]
+                    fine, coarse = delay & 127, delay >> 7
+                    keep_lanes = lane < 128 - fine
+                    for step in range(0, blocks, 8):
+                        start = (first + step - coarse - 1) & (all_blocks - 1)
+                        before = source[pl.ds(start * spread_rows + row, 8, stride=spread_rows), :]
+                        after = source[pl.ds((start + 1) * spread_rows + row, 8, stride=spread_rows), :]
+                        moved[pl.ds(step * spread_rows + row, 8, stride=spread_rows), :] = pltpu.roll(
+                            jnp.where(keep_lanes, after, before), fine, 1
+                        )
+                return carry
+
+            lax.fori_loop(0, depth // 4, shift_rows, 0)
+
+            def pack(i, carry):
+                for u in range(8):
+                    block = i * 8 + u
+                    volt_ref[first + block] = moved[pl.ds(block * spread_rows, depth), :].astype(volt_ref.dtype)
+                return carry
+
+            lax.fori_loop(0, blocks // 8, pack, 0)
+            for k in range(len(peers(side, n_low, n_high)[0])):
+                gather(side, k, chunk).start()
+        return carry
+
+    lax.fori_loop(0, chunks, shift_chunk, 0)
+
+    high, low = sta // n_low, lax.rem(sta, n_low)
+    for side, count in enumerate((n_low, n_high)):
+        wanted = lax.broadcasted_iota(jnp.int32, (weight_ref.shape[2], count * depth), 0)
+        column = lax.broadcasted_iota(jnp.int32, wanted.shape, 1)
+        picks = []
+        for part in range(2):
+            station = jnp.full(wanted.shape, -1, jnp.int32)
+            for k in range(count):
+                in_row = high * n_low + lax.rem(low - k + n_low, n_low)
+                in_column = lax.rem(high - k + n_high, n_high) * n_low + low
+                owner = (in_row, in_column)[side]
+                begin = k * depth + part * stations
+                inside = (column >= begin) & (column < begin + stations)
+                station = jnp.where(inside, column - begin + owner * stations, station)
+            picks.append((wanted == station).astype(jnp.float32).astype(jnp.bfloat16))
+        pick = lambda part, where: jnp.dot(weight_ref[part], picks[where], preferred_element_type=jnp.float32)
+        signed[0, :, : count * depth] = pick(0, 0) - pick(1, 1)
+        signed[1, :, : count * depth] = pick(1, 0) + pick(0, 1)
+        for k in range((n_high, n_low)[side]):
+            in_column = lax.rem(high + k, n_high) * n_low + low
+            in_row = high * n_low + lax.rem(low + k, n_low)
+            owner = (in_column, in_row)[side]
+            for part in range(2):
+                begin = (k * 2 + part) * n_beams
+                weight_refs[side][begin : begin + n_beams, :] = signed[
+                    part, pl.ds(owner * n_beams, n_beams), : count * depth
+                ]
 
     def turns(beam, carry):
-        measure = DM_STEP * dm_ref[beam, 0].astype(jnp.float32)
+        measure = DM_STEP * dm_ref[beam].astype(jnp.float32)
         for part in range(0, root, 64):
             chirp[beam, 0, part : part + 64], chirp[beam, 1, part : part + 64] = turn(
                 measure * base_ref[0, part : part + 64]
@@ -228,8 +256,8 @@
         for side in range(2):
             members = len(peers(side, n_low, n_high)[0])
             for k in range(members):
-                gathers[side, k, chunk].wait_recv()
-            weights = weight_refs[side][...]
+                gather(side, k, chunk).wait_recv()
+            weights = weight_refs[side][...].astype(jnp.bfloat16)
 
             def rows(i, carry):
                 for u in range(8):
@@ -401,8 +429,12 @@
         return carry
 
     lax.fori_loop(0, n_beams, drain, 0)
-    for copy in (*gathers.values(), *scales.values()):
+    for copy in scales.values():
         copy.wait_send()
+    for chunk in range(chunks):
+        for side in range(2):
+            for k in range(len(peers(side, n_low, n_high)[0])):
+                gather(side, k, chunk).wait_send()
     own_peak.wait()
     for k in range(1, n_sub):
         move_peak(k).wait_send()
@@ -420,8 +452,9 @@
     lax.fori_loop(0, n_beams, settle, 0)
 
 
-def make_series(dm_index, volts, weights, base_phase, n_low, n_high, n_sub, root):
-    blocks, depth, _ = volts.shape
+def make_series(dm_index, delays, volts, weights, base_phase, n_low, n_high, n_sub, root):
+    depth, blocks = 2 * volts.shape[1], volts.shape[2] // 128
+    spread_rows = depth + 4
     chunks = 4
     n_beams = dm_index.shape[0]
     half = root // 2
@@ -436,7 +469,7 @@
     per_side = lambda make: [make(*group) for group in groups]
     return pl.pallas_call(
         functools.partial(series_kernel, n_low, n_high, chunks),
-        in_specs=[pl.BlockSpec(memory_space=pltpu.SMEM), *[vmem] * 7],
+        in_specs=[*[pl.BlockSpec(memory_space=pltpu.SMEM)] * 2, *[vmem] * 6],
         out_specs=(hbm, hbm),
         out_shape=(
             jax.ShapeDtypeStruct((n_sta, n_beams, n_sub, 2, rows_out, 128), jnp.int16),
@@ -470,6 +503,11 @@
             dma((n_sta - 1,)),
             dma((n_sta - 1,)),
             dma((n_beams + 1,)),
+            *per_side(lambda g, r: pltpu.VMEM((r * 2 * n_beams, g * depth), jnp.float32)),
+            pltpu.VMEM((blocks, depth, 128), jnp.bfloat16),
+            pltpu.VMEM(((blocks + 16) * spread_rows, 128), jnp.float32),
+            pltpu.VMEM((blocks // 2 // chunks * spread_rows, 128), jnp.float32),
+            pltpu.VMEM((2, weights.shape[1], 128), jnp.float32),
         ],
         compiler_params=pltpu.CompilerParams(
             collective_id=0, has_side_effects=True, vmem_limit_bytes=60 * 1024 * 1024
@@ -477,27 +515,7 @@
         cost_estimate=pl.CostEstimate(
             flops=8 * n_beams * depth * blocks * 128, bytes_accessed=2 * volts.size, transcendentals=0
         ),
-    )(dm_index, volts, *weights, base_phase, *tables)
-
-
-def order_weights(own_weights, n_low, n_high, n_beams):
-    n_sta = n_low * n_high
-    w_real, w_imag = own_weights[0], own_weights[1]
-    full = jnp.stack([jnp.stack([w_real, -w_imag], axis=1), jnp.stack([w_imag, w_real], axis=1)])
-    full = full.reshape(2, n_sta, n_beams, 2, n_sta, -1)
-    sta = lax.axis_index("sta")
-    high, low = sta // n_low, lax.rem(sta, n_low)
-    in_row = lambda step, n: high * n_low + lax.rem(low + step * jnp.arange(n) + n, n)
-    in_column = lambda step, n: lax.rem(high + step * jnp.arange(n) + n, n) * n_low + low
-    out = []
-    for beam_ids, station_ids in (
-        (in_column(1, n_high), in_row(-1, n_low)),
-        (in_row(1, n_low), in_column(-1, n_high)),
-    ):
-        chosen = jnp.take(jnp.take(full, beam_ids, axis=1), station_ids, axis=4)
-        chosen = chosen.transpose(1, 0, 2, 4, 3, 5)
-        out.append(chosen.reshape(chosen.shape[0] * 2 * n_beams, -1))
-    return out
+    )(dm_index[:, 0], delays, volts, weights, base_phase, *tables)
 
 
 def shards(voltages, beam_weights, station_delays, dm_index):
@@ -511,11 +529,11 @@
     assert sub_dev == 1 and trials == 1 and root_len * root_len == total_len
     n_low = 2 if n_sta % 2 == 0 else 1
     n_high = n_sta // n_low
-    shifted = shift(voltages[0], station_delays)
-    weights = order_weights(beam_weights[0], n_low, n_high, local_beams)
     subband = lax.axis_index("sub") + jnp.arange(1, dtype=jnp.int32)
     base_phase = chirp_base(subband, root_len, total_len)
-    codes, peak = make_series(dm_index, shifted, weights, base_phase, n_low, n_high, n_sub, root_len)
+    codes, peak = make_series(
+        dm_index, station_delays, voltages[0], beam_weights[0], base_phase, n_low, n_high, n_sub, root_len
+    )
     peak = peak.transpose(1, 0, 2, 3)[:, None, :, :, None, :]
     moved = dequantize(codes.transpose(2, 3, 0, 1, 4, 5), peak)
     moved = moved.reshape(n_sub, 2, n_sta * local_beams, *moved.shape[4:])

time: 149 us -> 132 us (0.89)
  Pallas kernels: 134 us -> 123 us
  local copies, waits for them, and re-layouts: 8.56 us -> 2.66 us
    pallas_call x1 -> x0, Pallas kernels: 13.3 us -> none  [shift(): pl.pallas_call(shift_kernel, grid=(parts,), in_specs=[pl.BlockSpec(memory...]
    pallas_call x1, Pallas kernels: 120 us -> 123 us  [make_series(): pl.pallas_call(functools.partial(series_kernel, n_low, n_high, chunks), i...]
    gather x4 -> x0, local copies, waits for them, and re-layouts: 2.26 us -> none  [order_weights(): chosen = jnp.take(jnp.take(full, beam_ids, axis=1), station_ids, axis=4)]
    unnamed x2 -> x1, local copies, waits for them, and re-layouts: 3.95 us -> 2.63 us
where the time goes in v3:
time: 132 us; the launch traced here: 131 us
  Pallas kernels  123 us (93%)
  other arithmetic  5.11 us (4%)
  local copies, waits for them, and re-layouts  2.66 us (2%)
    pallas_call x1, Pallas kernels, make_series(): pl.pallas_call(functools.partial(series_kernel, n_low, n_high, chunks), i...  123 us

profile of v3, /device:TPU:0, one launch (start us, length us, event | category | flops | bytes accessed | tf_op | source)
XLA Modules:
  0.0 131.4 jit_solution(11757394564767432375)
XLA Ops:
  0.6 0.8 multiply_divide_fusion.base_ref
  1.5 122.9 %shard_map.86 = (s16[4,8,8,2,16,128]{5,4,3,2,1,0:T(8,128)(2,1)}, f32[4,8,8,128]{3,2,1,0:T(8,128)}) custom-call(s32[8]{0:T(128)} %bitcast.15, s32[16]{0:T(128)} %delay_ref.1, bf16[2,16,65536]{2,1,0:T(8,128)(2,1)} %bitcast.11, bf16[2,32,64]{2,1,0:T(8,128)(2,1)} %bitcast.14, f32[1,256,256]{2,1,0:T(8,128)} %multiply_divide_fusion.base_ref, ...), custom_call_target="tpu_custom_call" | custom-call | flops 134217728 | bytes 4194304 | tf_op jit(solution)/shard_map/pallas_call | solution.py:470
  124.4 0.9 multiply_bitcast_fusion
  125.4 2.4 %bitcast_multiply_fusion = f32[8,2,4,8,16,128]{5,4,1,0,3,2:T(8,128)S(1)} fusion(s16[4,8,8,2,16,128]{5,4,3,2,1,0:T(8,128)(2,1)} %get-tuple-element.4, f32[8,4,8,128]{3,0,2,1:T(8,128)S(1)} %copy.9), kind=kLoop, calls=%fused_computation | loop fusion | flops 3145728 | bytes 6422528 | tf_op jit(solution)/shard_map/mul | solution.py:71
  127.8 0.3 fusion.1
  128.0 0.7 broadcast_multiply_fusion
  128.8 2.6 %copy.11 = f32[8,2,4,8,16,128]{5,4,3,2,1,0:T(8,128)} copy(f32[8,2,4,8,16,128]{5,4,1,0,3,2:T(8,128)S(1)} %bitcast_multiply_fusion) | data formatting | bytes 8388608
  (2 shorter events, 0.0 us)

commit v4 on v3

--- a/solution.py
+++ b/solution.py
@@ -117,9 +117,9 @@
     raw_ref,
     weight_ref,
     base_ref,
-    left_ref,
-    right_ref,
-    twist_ref,
+    left_hbm,
+    right_hbm,
+    twist_hbm,
     out_ref,
     peak_ref,
     *scratch,
@@ -129,10 +129,16 @@
         scratch[12 + 2 * i : 14 + 2 * i] for i in range(6)
     )
     chirp, flat, ready, ready_peak, middle, middle_peak = scratch[24:30]
-    weight_refs, volt_ref, source, moved, signed = scratch[39:41], *scratch[41:]
+    weight_refs, volt_ref, source, moved, signed = scratch[39:41], *scratch[41:45]
+    left_ref, right_ref, twist_ref, table_sem = scratch[45:]
+    tables = [
+        pltpu.make_async_copy(left_hbm, left_ref, table_sem.at[0]),
+        pltpu.make_async_copy(right_hbm, right_ref, table_sem.at[1]),
+        pltpu.make_async_copy(twist_hbm, twist_ref, table_sem.at[2]),
+    ]
     move_send, move_recv, peak_send, peak_recv, pass_send, pass_recv, last_send, last_recv, own_sem = scratch[30:39]
     n_sta, n_beams, n_sub, _, rows_out, _ = out_ref.shape
-    root = twist_ref.shape[1]
+    root = twist_hbm.shape[1]
     n_dev = n_sub * n_sta
     sub, sta = lax.axis_index("sub"), lax.axis_index("sta")
     sub_peer = lambda k: lax.rem(sub + k, n_sub)
@@ -147,7 +153,8 @@
         pl.semaphore_signal(barrier, inc=1, device_id=(sub_peer(k), sta), device_id_type=MESH)
     for k in range(1, n_sta):
         pl.semaphore_signal(barrier, inc=1, device_id=(sub, sta_peer(k)), device_id_type=MESH)
-    pl.semaphore_wait(barrier, n_sub + n_sta - 2)
+    for copy in tables:
+        copy.start()
 
     stations, total_len = raw_ref.shape[1:]
     depth = 2 * stations
@@ -169,12 +176,13 @@
             pl.ds(block * spread_rows, depth), :
         ]
     lane = lax.broadcasted_iota(jnp.int32, (8, 128), 1)
+    pl.semaphore_wait(barrier, n_sub + n_sta - 2)
 
     def gather(side, k, chunk):
         return pltpu.make_async_remote_copy(
             src_ref=volt_ref.at[pl.ds((side * chunks + chunk) * blocks, blocks)],
             dst_ref=got[side].at[k, pl.ds(chunk * blocks, blocks)],
-            send_sem=gather_send[side].at[k, chunk],
+            send_sem=gather_send[side].at[k],
             recv_sem=gather_recv[side].at[k, chunk],
             device_id=peers(side, n_low, n_high)[0][k],
             device_id_type=MESH,
@@ -280,101 +288,96 @@
     def piece(side, k, part, beam, lanes):
         return partial[side][lanes, pl.ds(((k * 2 + part) * n_beams + beam) * pitch, half), :]
 
-    for side in range(2):
-        for k in range(len(peers(side, n_low, n_high)[1])):
-
-            def encode(beam, carry):
+    def exchange(side, k, beam):
+        return pltpu.make_async_remote_copy(
+            src_ref=codes[side].at[k, beam],
+            dst_ref=landed[side].at[k, beam],
+            send_sem=sum_send[side].at[k],
+            recv_sem=sum_recv[side].at[k, beam],
+            device_id=peers(side, n_low, n_high)[1][k],
+            device_id_type=MESH,
+        )
+
+    def exchange_scale(side, k, beam):
+        return pltpu.make_async_remote_copy(
+            src_ref=scale[side].at[k, beam],
+            dst_ref=scale_in[side].at[k, beam],
+            send_sem=scale_send[side].at[k],
+            recv_sem=scale_recv[side].at[k, beam],
+            device_id=peers(side, n_low, n_high)[1][k],
+            device_id_type=MESH,
+        )
+
+    def encode(beam, carry):
+        for side in range(2):
+            for k in range(len(peers(side, n_low, n_high)[1])):
                 for lanes in range(2):
                     values = [piece(side, k + 1, part, beam, lanes) for part in range(2)]
                     ceiling = jnp.max(jnp.maximum(jnp.abs(values[0]), jnp.abs(values[1])), axis=0, keepdims=True)
                     scale[side][k, beam, lanes : lanes + 1, :] = ceiling
                     for part in range(2):
                         codes[side][k, beam, part, lanes] = quantize(values[part], ceiling)
-                return carry
-
-            lax.fori_loop(0, n_beams, encode, 0)
-
-    scales = {}
-    for side in range(2):
-        for k, peer in enumerate(peers(side, n_low, n_high)[1]):
-            scales[side, k] = pltpu.make_async_remote_copy(
-                src_ref=scale[side].at[k],
-                dst_ref=scale_in[side].at[k],
-                send_sem=scale_send[side].at[k],
-                recv_sem=scale_recv[side].at[k],
-                device_id=peer,
-                device_id_type=MESH,
-            )
-            scales[side, k].start()
-
-    def exchange(side, k, beam):
-        return pltpu.make_async_remote_copy(
-            src_ref=codes[side].at[k, beam],
-            dst_ref=landed[side].at[k, beam],
-            send_sem=sum_send[side].at[k, beam],
-            recv_sem=sum_recv[side].at[k, beam],
-            device_id=peers(side, n_low, n_high)[1][k],
-            device_id_type=MESH,
-        )
-
-    def each_exchange(beam, act):
+                exchange_scale(side, k, beam).start()
+                exchange(side, k, beam).start()
+        return carry
+
+    lax.fori_loop(0, n_beams, encode, 0)
+    for copy in tables:
+        copy.wait()
+
+    def total_of(ref, send_sem, recv_sem):
+        return pltpu.make_async_remote_copy(
+            src_ref=ref, dst_ref=ref, send_sem=send_sem, recv_sem=recv_sem, device_id=(sub, sta), device_id_type=MESH
+        )
+
+    def move(beam, k):
+        return pltpu.make_async_remote_copy(
+            src_ref=ready.at[sub_peer(k), beam],
+            dst_ref=middle.at[beam, sub],
+            send_sem=move_send.at[k - 1],
+            recv_sem=move_recv.at[beam],
+            device_id=(sub_peer(k), sta),
+            device_id_type=MESH,
+        )
+
+    def move_peak(k):
+        return pltpu.make_async_remote_copy(
+            src_ref=ready_peak,
+            dst_ref=middle_peak.at[sub],
+            send_sem=peak_send,
+            recv_sem=peak_recv,
+            device_id=(sub_peer(k), sta),
+            device_id_type=MESH,
+        )
+
+    def forward(beam, k):
+        return pltpu.make_async_remote_copy(
+            src_ref=middle.at[beam, :, sta_peer(k)],
+            dst_ref=out_ref.at[sta, beam],
+            send_sem=pass_send.at[k - 1],
+            recv_sem=pass_recv.at[k - 1],
+            device_id=(sub, sta_peer(k)),
+            device_id_type=MESH,
+        )
+
+    def forward_peak(k):
+        return pltpu.make_async_remote_copy(
+            src_ref=middle_peak,
+            dst_ref=peak_ref.at[sta],
+            send_sem=last_send,
+            recv_sem=last_recv,
+            device_id=(sub, sta_peer(k)),
+            device_id_type=MESH,
+        )
+
+    def keep(beam):
+        return pltpu.make_async_copy(middle.at[beam, :, sta], out_ref.at[sta, beam], own_sem.at[0])
+
+    def finish(beam, carry):
         for side in range(2):
             for k in range(len(peers(side, n_low, n_high)[1])):
-                act(exchange(side, k, beam))
-
-    def launch(beam, carry):
-        each_exchange(beam, lambda copy: copy.start())
-        return carry
-
-    lax.fori_loop(0, n_beams, launch, 0)
-    for copy in scales.values():
-        copy.wait_recv()
-
-    def move(beam, k):
-        return pltpu.make_async_remote_copy(
-            src_ref=ready.at[sub_peer(k), beam],
-            dst_ref=middle.at[beam, sub],
-            send_sem=move_send.at[beam, k - 1],
-            recv_sem=move_recv.at[beam, k - 1],
-            device_id=(sub_peer(k), sta),
-            device_id_type=MESH,
-        )
-
-    def move_peak(k):
-        return pltpu.make_async_remote_copy(
-            src_ref=ready_peak,
-            dst_ref=middle_peak.at[sub],
-            send_sem=peak_send.at[k - 1],
-            recv_sem=peak_recv.at[k - 1],
-            device_id=(sub_peer(k), sta),
-            device_id_type=MESH,
-        )
-
-    def forward(beam, k):
-        return pltpu.make_async_remote_copy(
-            src_ref=middle.at[beam, :, sta_peer(k)],
-            dst_ref=out_ref.at[sta, beam],
-            send_sem=pass_send.at[beam, k - 1],
-            recv_sem=pass_recv.at[beam, k - 1],
-            device_id=(sub, sta_peer(k)),
-            device_id_type=MESH,
-        )
-
-    def forward_peak(k):
-        return pltpu.make_async_remote_copy(
-            src_ref=middle_peak,
-            dst_ref=peak_ref.at[sta],
-            send_sem=last_send.at[k - 1],
-            recv_sem=last_recv.at[k - 1],
-            device_id=(sub, sta_peer(k)),
-            device_id_type=MESH,
-        )
-
-    def keep(beam):
-        return pltpu.make_async_copy(middle.at[beam, :, sta], out_ref.at[sta, beam], own_sem.at[beam])
-
-    def finish(beam, carry):
-        each_exchange(beam, lambda copy: copy.wait_recv())
+                exchange_scale(side, k, beam).wait_recv()
+                exchange(side, k, beam).wait_recv()
         quarters = []
         for part in range(2):
             for side in range(2):
@@ -409,53 +412,43 @@
         move_peak(k).start()
 
     def spread(beam, carry):
-        for k in range(1, n_sub):
-            move(beam, k).wait_recv()
+        total_of(middle.at[beam, pl.ds(0, n_sub - 1)], move_send.at[0], move_recv.at[beam]).wait_recv()
         for k in range(1, n_sta):
             forward(beam, k).start()
         keep(beam).start()
         return carry
 
     lax.fori_loop(0, n_beams, spread, 0)
-    for k in range(1, n_sub):
-        move_peak(k).wait_recv()
+    arrived = middle_peak.at[pl.ds(0, n_sub - 1)]
+    total_of(arrived, peak_send, peak_recv).wait_recv()
     for k in range(1, n_sta):
         forward_peak(k).start()
-    own_peak = pltpu.make_async_copy(middle_peak, peak_ref.at[sta], own_sem.at[n_beams])
+    own_peak = pltpu.make_async_copy(middle_peak, peak_ref.at[sta], own_sem.at[1])
     own_peak.start()
 
-    def drain(beam, carry):
-        each_exchange(beam, lambda copy: copy.wait_send())
-        return carry
-
-    lax.fori_loop(0, n_beams, drain, 0)
-    for copy in scales.values():
-        copy.wait_send()
-    for chunk in range(chunks):
-        for side in range(2):
-            for k in range(len(peers(side, n_low, n_high)[0])):
-                gather(side, k, chunk).wait_send()
+    for side in range(2):
+        whole = volt_ref.at[pl.ds(side * chunks * blocks, chunks * blocks)]
+        for k in range(len(peers(side, n_low, n_high)[0])):
+            total_of(whole, gather_send[side].at[k], gather_send[side].at[k]).wait_send()
+        for k in range(len(peers(side, n_low, n_high)[1])):
+            total_of(codes[side].at[k], sum_send[side].at[k], sum_send[side].at[k]).wait_send()
+            total_of(scale[side].at[k], scale_send[side].at[k], scale_send[side].at[k]).wait_send()
+    for k in range(1, n_sub):
+        total_of(ready.at[sub_peer(k)], move_send.at[k - 1], move_send.at[k - 1]).wait_send()
+    total_of(arrived, peak_send, peak_recv).wait_send()
+    pltpu.make_async_copy(middle.at[:, :, sta], out_ref.at[sta], own_sem.at[0]).wait()
     own_peak.wait()
-    for k in range(1, n_sub):
-        move_peak(k).wait_send()
     for k in range(1, n_sta):
-        forward_peak(k).wait()
-
-    def settle(beam, carry):
-        keep(beam).wait()
-        for k in range(1, n_sub):
-            move(beam, k).wait_send()
-        for k in range(1, n_sta):
-            forward(beam, k).wait()
-        return carry
-
-    lax.fori_loop(0, n_beams, settle, 0)
+        total_of(middle.at[:, :, sta_peer(k)], pass_send.at[k - 1], pass_recv.at[k - 1]).wait_send()
+        total_of(out_ref.at[sta_peer(k)], pass_send.at[k - 1], pass_recv.at[k - 1]).wait_recv()
+    others = peak_ref.at[pl.ds(0, n_sta - 1)]
+    total_of(others, last_send, last_recv).wait()
 
 
 def make_series(dm_index, delays, volts, weights, base_phase, n_low, n_high, n_sub, root):
     depth, blocks = 2 * volts.shape[1], volts.shape[2] // 128
     spread_rows = depth + 4
-    chunks = 4
+    chunks = 8
     n_beams = dm_index.shape[0]
     half = root // 2
     n_sta = n_low * n_high
@@ -469,7 +462,7 @@
     per_side = lambda make: [make(*group) for group in groups]
     return pl.pallas_call(
         functools.partial(series_kernel, n_low, n_high, chunks),
-        in_specs=[*[pl.BlockSpec(memory_space=pltpu.SMEM)] * 2, *[vmem] * 6],
+        in_specs=[*[pl.BlockSpec(memory_space=pltpu.SMEM)] * 2, *[vmem] * 3, *[hbm] * 3],
         out_specs=(hbm, hbm),
         out_shape=(
             jax.ShapeDtypeStruct((n_sta, n_beams, n_sub, 2, rows_out, 128), jnp.int16),
@@ -482,32 +475,34 @@
             *per_side(lambda g, r: pltpu.VMEM((r - 1, n_beams, 2, 2, half, 128), jnp.int16)),
             *per_side(lambda g, r: pltpu.VMEM((r - 1, n_beams, 8, 128), jnp.float32)),
             *per_side(lambda g, r: pltpu.VMEM((r - 1, n_beams, 8, 128), jnp.float32)),
+            *per_side(lambda g, r: dma((g - 1,))),
             *per_side(lambda g, r: dma((g - 1, chunks))),
-            *per_side(lambda g, r: dma((g - 1, chunks))),
-            *per_side(lambda g, r: dma((r - 1, n_beams))),
+            *per_side(lambda g, r: dma((r - 1,))),
             *per_side(lambda g, r: dma((r - 1, n_beams))),
             *per_side(lambda g, r: dma((r - 1,))),
-            *per_side(lambda g, r: dma((r - 1,))),
+            *per_side(lambda g, r: dma((r - 1, n_beams))),
             pltpu.VMEM((n_beams, 2, root, root), jnp.float32),
             pltpu.VMEM((2, 2 * root, 128), jnp.float32),
             pltpu.VMEM((n_sub, n_beams, n_sta, 2, rows_out, 128), jnp.int16),
             pltpu.VMEM((n_beams, 128), jnp.float32),
             pltpu.VMEM((n_beams, n_sub, n_sta, 2, rows_out, 128), jnp.int16),
             pltpu.VMEM((n_sub, n_beams, 128), jnp.float32),
-            dma((n_beams, n_sub - 1)),
-            dma((n_beams, n_sub - 1)),
             dma((n_sub - 1,)),
-            dma((n_sub - 1,)),
-            dma((n_beams, n_sta - 1)),
-            dma((n_beams, n_sta - 1)),
+            dma((n_beams,)),
+            dma,
+            dma,
             dma((n_sta - 1,)),
             dma((n_sta - 1,)),
-            dma((n_beams + 1,)),
+            dma,
+            dma,
+            dma((2,)),
             *per_side(lambda g, r: pltpu.VMEM((r * 2 * n_beams, g * depth), jnp.float32)),
             pltpu.VMEM((blocks, depth, 128), jnp.bfloat16),
             pltpu.VMEM(((blocks + 16) * spread_rows, 128), jnp.float32),
             pltpu.VMEM((blocks // 2 // chunks * spread_rows, 128), jnp.float32),
             pltpu.VMEM((2, weights.shape[1], 128), jnp.float32),
+            *[pltpu.VMEM(table.shape, table.dtype) for table in tables],
+            dma((3,)),
         ],
         compiler_params=pltpu.CompilerParams(
             collective_id=0, has_side_effects=True, vmem_limit_bytes=60 * 1024 * 1024
@@ -516,6 +511,38 @@
             flops=8 * n_beams * depth * blocks * 128, bytes_accessed=2 * volts.size, transcendentals=0
         ),
     )(dm_index[:, 0], delays, volts, weights, base_phase, *tables)
+
+
+def unpack_kernel(codes_ref, peak_ref, out_ref, power_ref):
+    n_sub, _, n_beams = out_ref.shape[:3]
+    for beam in range(n_beams):
+        power = jnp.zeros(power_ref.shape[1:], jnp.float32)
+        for sub in range(n_sub):
+            for part in range(2):
+                values = dequantize(codes_ref[0, beam, sub, part], peak_ref[0, sub, beam : beam + 1, :])
+                out_ref[sub, part, beam] = values
+                power = power + values * values
+        power_ref[beam] = power * (1.0 / n_sub)
+
+
+def unpack_series(codes, peak):
+    n_sta, n_beams, n_sub, _, rows, lanes = codes.shape
+    return pl.pallas_call(
+        unpack_kernel,
+        grid=(n_sta,),
+        in_specs=[
+            pl.BlockSpec((1, n_beams, n_sub, 2, rows, lanes), lambda i: (i, 0, 0, 0, 0, 0)),
+            pl.BlockSpec((1, n_sub, n_beams, lanes), lambda i: (i, 0, 0, 0)),
+        ],
+        out_specs=[
+            pl.BlockSpec((n_sub, 2, n_beams, rows, lanes), lambda i: (0, 0, i, 0, 0)),
+            pl.BlockSpec((n_beams, rows, lanes), lambda i: (i, 0, 0)),
+        ],
+        out_shape=[
+            jax.ShapeDtypeStruct((n_sub, 2, n_sta * n_beams, rows, lanes), jnp.float32),
+            jax.ShapeDtypeStruct((n_sta * n_beams, rows, lanes), jnp.float32),
+        ],
+    )(codes, peak)
 
 
 def shards(voltages, beam_weights, station_delays, dm_index):
@@ -534,10 +561,7 @@
     codes, peak = make_series(
         dm_index, station_delays, voltages[0], beam_weights[0], base_phase, n_low, n_high, n_sub, root_len
     )
-    peak = peak.transpose(1, 0, 2, 3)[:, None, :, :, None, :]
-    moved = dequantize(codes.transpose(2, 3, 0, 1, 4, 5), peak)
-    moved = moved.reshape(n_sub, 2, n_sta * local_beams, *moved.shape[4:])
-    intensity = jnp.mean(moved[:, 0] * moved[:, 0] + moved[:, 1] * moved[:, 1], axis=0)
+    moved, intensity = unpack_series(codes, peak)
     return (moved.reshape(*moved.shape[:3], 1, -1), intensity.reshape(intensity.shape[0], 1, -1))
 
 

time: 132 us -> 123 us (0.932)
  other arithmetic: 5.11 us -> 0.83 us
  local copies, waits for them, and re-layouts: 2.66 us -> 0 us
    pallas_call x1, Pallas kernels: 123 us -> 117 us  [make_series(): pl.pallas_call(functools.partial(series_kernel, n_low, n_high, chunks), i...]
    pallas_call x0 -> x1, Pallas kernels: none -> 4.47 us  [unpack_series(): pl.pallas_call(unpack_kernel, grid=(n_sta,), in_specs=[pl.BlockSpec((1, n...]
    mul x2 -> x0, other arithmetic: 3.29 us -> none  [the longest x1 2.37 us: dequantize(): codes.astype(jnp.int32).astype(jnp.float32) * (ceiling * (1.0 / PEAK))]
    unnamed x1 -> x0, local copies, waits for them, and re-layouts: 2.63 us -> none
where the time goes in v4:
time: 123 us
  Pallas kernels  122 us (99%)
    pallas_call x1, Pallas kernels, make_series(): pl.pallas_call(functools.partial(series_kernel, n_low, n_high, chunks), i...  117 us
    pallas_call x1, Pallas kernels, unpack_series(): pl.pallas_call(unpack_kernel, grid=(n_sta,), in_specs=[pl.BlockSpec((1, n...  4.47 us

profile of v4, /device:TPU:0, one launch (start us, length us, event | category | flops | bytes accessed | tf_op | source)
XLA Modules:
  0.0 123.0 jit_solution(9709561513496451194)
XLA Ops:
  0.6 0.8 multiply_divide_fusion.base_ref
  1.5 117.0 %shard_map.86 = (s16[4,8,8,2,16,128]{5,4,3,2,1,0:T(8,128)(2,1)}, f32[4,8,8,128]{3,2,1,0:T(8,128)}) custom-call(s32[8]{0:T(128)} %bitcast.7, s32[16]{0:T(128)} %delay_ref.1, bf16[2,16,65536]{2,1,0:T(8,128)(2,1)} %bitcast.5, bf16[2,32,64]{2,1,0:T(8,128)(2,1)} %bitcast.6, f32[1,256,256]{2,1,0:T(8,128)} %multiply_divide_fusion.base_ref, ...), custom_call_target="tpu_custom_call" | custom-call | flops 134217728 | bytes 4194304 | tf_op jit(solution)/shard_map/pallas_call | solution.py:463
  118.5 4.5 %shard_map.87 = (f32[8,2,32,16,128]{4,3,2,1,0:T(8,128)}, f32[32,16,128]{2,1,0:T(8,128)}) custom-call(s16[4,8,8,2,16,128]{5,4,3,2,1,0:T(8,128)(2,1)} %get-tuple-element.6.codes_ref, f32[4,8,8,128]{3,2,1,0:T(8,128)} %get-tuple-element.7.peak_ref), custom_call_target="tpu_custom_call" | custom-call | tf_op jit(solution)/shard_map/pallas_call | solution.py:530
  (1 shorter events, 0.0 us)

commit v5 on v4

--- a/solution.py
+++ b/solution.py
@@ -29,13 +29,15 @@
     return np.stack([high, low]), np.stack([high.T, low.T]), twist
 
 
-def chirp_base(subband, root_len, total_len):
-    first = jnp.arange(root_len, dtype=jnp.int32)[:, None]
-    second = jnp.arange(root_len, dtype=jnp.int32)[None, :]
+def chirp_base(subband, begin, rows, root_len):
+    total_len = root_len * root_len
+    first = lax.broadcasted_iota(jnp.int32, (rows, root_len), 0) + begin
+    second = lax.broadcasted_iota(jnp.int32, (rows, root_len), 1)
     positions = first + root_len * second
     signed_bin = jnp.where(positions < total_len // 2, positions, positions - total_len)
-    offset = (CHANNEL_WIDTH * signed_bin.astype(jnp.float32) / total_len)[None]
-    centre = (BASE_FREQ + CHANNEL_WIDTH * (subband.astype(jnp.float32) + 0.5))[:, None, None]
+    offset = CHANNEL_WIDTH * signed_bin.astype(jnp.float32) / total_len
+    band = jnp.full((rows, root_len), subband, jnp.int32).astype(jnp.float32)
+    centre = BASE_FREQ + CHANNEL_WIDTH * (band + 0.5)
     return TWO_PI * DISPERSION * offset * offset / (centre * centre * (centre + offset))
 
 
@@ -114,9 +116,8 @@
     chunks,
     dm_ref,
     delay_ref,
-    raw_ref,
+    raw_hbm,
     weight_ref,
-    base_ref,
     left_hbm,
     right_hbm,
     twist_hbm,
@@ -130,7 +131,7 @@
     )
     chirp, flat, ready, ready_peak, middle, middle_peak = scratch[24:30]
     weight_refs, volt_ref, source, moved, signed = scratch[39:41], *scratch[41:45]
-    left_ref, right_ref, twist_ref, table_sem = scratch[45:]
+    left_ref, right_ref, twist_ref, table_sem, raw_ref, raw_sem = scratch[45:]
     tables = [
         pltpu.make_async_copy(left_hbm, left_ref, table_sem.at[0]),
         pltpu.make_async_copy(right_hbm, right_ref, table_sem.at[1]),
@@ -147,16 +148,25 @@
     pitch = partial[0].shape[1] // weight_refs[0].shape[0]
     blocks = volt_ref.shape[0] // 2 // chunks
 
+    quarter = raw_hbm.shape[2] // 4
+
+    def fetch(index):
+        span = pl.ds(index * quarter, quarter)
+        return pltpu.make_async_copy(raw_hbm.at[:, :, span], raw_ref.at[:, :, span], raw_sem.at[index])
+
+    for index in (3, 0, 1, 2):
+        fetch(index).start()
+    for copy in tables:
+        copy.start()
+
     barrier = pltpu.get_barrier_semaphore()
 
     for k in range(1, n_sub):
         pl.semaphore_signal(barrier, inc=1, device_id=(sub_peer(k), sta), device_id_type=MESH)
     for k in range(1, n_sta):
         pl.semaphore_signal(barrier, inc=1, device_id=(sub, sta_peer(k)), device_id_type=MESH)
-    for copy in tables:
-        copy.start()
-
-    stations, total_len = raw_ref.shape[1:]
+
+    stations, total_len = raw_hbm.shape[1:]
     depth = 2 * stations
     spread_rows = depth + 4
     all_blocks = total_len // 128
@@ -170,7 +180,15 @@
                 ].astype(jnp.float32)
         return carry
 
-    lax.fori_loop(0, all_blocks // 8, unpack, 0)
+    unit = all_blocks // 16
+
+    def unpack_units(first, last):
+        lax.fori_loop(first * unit // 8, last * unit // 8, unpack, 0)
+
+    fetch(3).wait()
+    unpack_units(12, 16)
+    fetch(0).wait()
+    unpack_units(0, 1)
     for block in range(16):
         source[pl.ds((all_blocks + block) * spread_rows, depth), :] = source[
             pl.ds(block * spread_rows, depth), :
@@ -188,39 +206,51 @@
             device_id_type=MESH,
         )
 
-    def shift_chunk(chunk, carry):
+    def shift_chunk(chunk, side):
+        first = (side * chunks + chunk) * blocks
+
+        def shift_rows(i, carry):
+            for u in range(4):
+                row = i * 4 + u
+                delay = delay_ref[row & (stations - 1)]
+                fine, coarse = delay & 127, delay >> 7
+                keep_lanes = lane < 128 - fine
+                for step in range(0, blocks, 8):
+                    start = (first + step - coarse - 1) & (all_blocks - 1)
+                    before = source[pl.ds(start * spread_rows + row, 8, stride=spread_rows), :]
+                    after = source[pl.ds((start + 1) * spread_rows + row, 8, stride=spread_rows), :]
+                    moved[pl.ds(step * spread_rows + row, 8, stride=spread_rows), :] = pltpu.roll(
+                        jnp.where(keep_lanes, after, before), fine, 1
+                    )
+            return carry
+
+        lax.fori_loop(0, depth // 4, shift_rows, 0)
+
+        def pack(i, carry):
+            for u in range(8):
+                block = i * 8 + u
+                volt_ref[first + block] = moved[pl.ds(block * spread_rows, depth), :].astype(volt_ref.dtype)
+            return carry
+
+        lax.fori_loop(0, blocks // 8, pack, 0)
+        for k in range(len(peers(side, n_low, n_high)[0])):
+            gather(side, k, chunk).start()
+
+    shift_chunk(0, 0)
+    fetch(1).wait()
+    unpack_units(4, 8)
+    fetch(2).wait()
+    unpack_units(8, 9)
+    shift_chunk(0, 1)
+    unpack_units(1, 4)
+    unpack_units(9, 12)
+
+    def shift_pair(chunk, carry):
         for side in range(2):
-            first = (side * chunks + chunk) * blocks
-
-            def shift_rows(i, carry):
-                for u in range(4):
-                    row = i * 4 + u
-                    delay = delay_ref[row & (stations - 1)]
-                    fine, coarse = delay & 127, delay >> 7
-                    keep_lanes = lane < 128 - fine
-                    for step in range(0, blocks, 8):
-                        start = (first + step - coarse - 1) & (all_blocks - 1)
-                        before = source[pl.ds(start * spread_rows + row, 8, stride=spread_rows), :]
-                        after = source[pl.ds((start + 1) * spread_rows + row, 8, stride=spread_rows), :]
-                        moved[pl.ds(step * spread_rows + row, 8, stride=spread_rows), :] = pltpu.roll(
-                            jnp.where(keep_lanes, after, before), fine, 1
-                        )
-                return carry
-
-            lax.fori_loop(0, depth // 4, shift_rows, 0)
-
-            def pack(i, carry):
-                for u in range(8):
-                    block = i * 8 + u
-                    volt_ref[first + block] = moved[pl.ds(block * spread_rows, depth), :].astype(volt_ref.dtype)
-                return carry
-
-            lax.fori_loop(0, blocks // 8, pack, 0)
-            for k in range(len(peers(side, n_low, n_high)[0])):
-                gather(side, k, chunk).start()
+            shift_chunk(chunk, side)
         return carry
 
-    lax.fori_loop(0, chunks, shift_chunk, 0)
+    lax.fori_loop(1, chunks, shift_pair, 0)
 
     high, low = sta // n_low, lax.rem(sta, n_low)
     for side, count in enumerate((n_low, n_high)):
@@ -250,15 +280,62 @@
                     part, pl.ds(owner * n_beams, n_beams), : count * depth
                 ]
 
-    def turns(beam, carry):
-        measure = DM_STEP * dm_ref[beam].astype(jnp.float32)
-        for part in range(0, root, 64):
-            chirp[beam, 0, part : part + 64], chirp[beam, 1, part : part + 64] = turn(
-                measure * base_ref[0, part : part + 64]
-            )
-        return carry
-
-    lax.fori_loop(0, n_beams, turns, 0)
+    for part in range(0, root, 64):
+        base_phase = chirp_base(sub, part, 64, root)
+
+        def turns(beam, carry):
+            measure = DM_STEP * dm_ref[beam].astype(jnp.float32)
+            chirp[beam, 0, part : part + 64], chirp[beam, 1, part : part + 64] = turn(measure * base_phase)
+            return carry
+
+        lax.fori_loop(0, n_beams, turns, 0)
+
+    def piece(side, k, part, beam, lanes):
+        return partial[side][lanes, pl.ds(((k * 2 + part) * n_beams + beam) * pitch, half), :]
+
+    def exchange(side, k, beam):
+        return pltpu.make_async_remote_copy(
+            src_ref=codes[side].at[k, beam],
+            dst_ref=landed[side].at[k, beam],
+            send_sem=sum_send[side].at[k],
+            recv_sem=sum_recv[side].at[k, beam],
+            device_id=peers(side, n_low, n_high)[1][k],
+            device_id_type=MESH,
+        )
+
+    def exchange_scale(side, k, beam):
+        return pltpu.make_async_remote_copy(
+            src_ref=scale[side].at[k, beam],
+            dst_ref=scale_in[side].at[k, beam],
+            send_sem=scale_send[side].at[k],
+            recv_sem=scale_recv[side].at[k, beam],
+            device_id=peers(side, n_low, n_high)[1][k],
+            device_id_type=MESH,
+        )
+
+    def encode_rows(side, k, beam, chunk):
+        tall = half // chunks
+        rows = pl.ds(chunk * tall, tall)
+        for lanes in range(2):
+            values = []
+            for part in range(2):
+                row = (((k + 1) * 2 + part) * n_beams + beam) * pitch + chunk * tall
+                values.append(partial[side][lanes, pl.ds(row, tall), :])
+            ceiling = jnp.max(jnp.maximum(jnp.abs(values[0]), jnp.abs(values[1])), axis=0, keepdims=True)
+            scale[side][k, beam, lanes, chunk : chunk + 1, :] = ceiling
+            for part in range(2):
+                codes[side][k, beam, part, lanes, rows, :] = quantize(values[part], ceiling)
+
+    def exchange_rows(side, k, chunk):
+        rows = pl.ds(chunk * (half // chunks), half // chunks)
+        return pltpu.make_async_remote_copy(
+            src_ref=codes[side].at[k, 0, :, :, rows],
+            dst_ref=landed[side].at[k, 0, :, :, rows],
+            send_sem=sum_send[side].at[k],
+            recv_sem=sum_recv[side].at[k, 0],
+            device_id=peers(side, n_low, n_high)[1][k],
+            device_id_type=MESH,
+        )
 
     for chunk in range(chunks):
         for side in range(2):
@@ -284,44 +361,24 @@
                 return carry
 
             lax.fori_loop(0, blocks // 16, rows, 0)
-
-    def piece(side, k, part, beam, lanes):
-        return partial[side][lanes, pl.ds(((k * 2 + part) * n_beams + beam) * pitch, half), :]
-
-    def exchange(side, k, beam):
-        return pltpu.make_async_remote_copy(
-            src_ref=codes[side].at[k, beam],
-            dst_ref=landed[side].at[k, beam],
-            send_sem=sum_send[side].at[k],
-            recv_sem=sum_recv[side].at[k, beam],
-            device_id=peers(side, n_low, n_high)[1][k],
-            device_id_type=MESH,
-        )
-
-    def exchange_scale(side, k, beam):
-        return pltpu.make_async_remote_copy(
-            src_ref=scale[side].at[k, beam],
-            dst_ref=scale_in[side].at[k, beam],
-            send_sem=scale_send[side].at[k],
-            recv_sem=scale_recv[side].at[k, beam],
-            device_id=peers(side, n_low, n_high)[1][k],
-            device_id_type=MESH,
-        )
+            for k in range(len(peers(side, n_low, n_high)[1])):
+                encode_rows(side, k, 0, chunk)
+                exchange_rows(side, k, chunk).start()
+
+    for side in range(2):
+        for k in range(len(peers(side, n_low, n_high)[1])):
+            exchange_scale(side, k, 0).start()
 
     def encode(beam, carry):
         for side in range(2):
             for k in range(len(peers(side, n_low, n_high)[1])):
-                for lanes in range(2):
-                    values = [piece(side, k + 1, part, beam, lanes) for part in range(2)]
-                    ceiling = jnp.max(jnp.maximum(jnp.abs(values[0]), jnp.abs(values[1])), axis=0, keepdims=True)
-                    scale[side][k, beam, lanes : lanes + 1, :] = ceiling
-                    for part in range(2):
-                        codes[side][k, beam, part, lanes] = quantize(values[part], ceiling)
+                for chunk in range(chunks):
+                    encode_rows(side, k, beam, chunk)
                 exchange_scale(side, k, beam).start()
                 exchange(side, k, beam).start()
         return carry
 
-    lax.fori_loop(0, n_beams, encode, 0)
+    lax.fori_loop(1, n_beams, encode, 0)
     for copy in tables:
         copy.wait()
 
@@ -385,8 +442,13 @@
                 for lanes in range(2):
                     total = piece(side, 0, part, beam, lanes)
                     for k in range(len(peers(side, n_low, n_high)[1])):
-                        ceiling = scale_in[side][k, beam, lanes : lanes + 1, :]
-                        total = total + dequantize(landed[side][k, beam, part, lanes], ceiling)
+                        pieces = []
+                        for chunk in range(chunks):
+                            tall = half // chunks
+                            ceiling = scale_in[side][k, beam, lanes, chunk : chunk + 1, :]
+                            rows = pl.ds(chunk * tall, tall)
+                            pieces.append(dequantize(landed[side][k, beam, part, lanes, rows, :], ceiling))
+                        total = total + jnp.concatenate(pieces, axis=0)
                     pair.append(total)
                 quarters.append(jnp.concatenate(pair, axis=1))
         x = jnp.concatenate(quarters, axis=0)
@@ -445,7 +507,7 @@
     total_of(others, last_send, last_recv).wait()
 
 
-def make_series(dm_index, delays, volts, weights, base_phase, n_low, n_high, n_sub, root):
+def make_series(dm_index, delays, volts, weights, n_low, n_high, n_sub, root):
     depth, blocks = 2 * volts.shape[1], volts.shape[2] // 128
     spread_rows = depth + 4
     chunks = 8
@@ -462,7 +524,7 @@
     per_side = lambda make: [make(*group) for group in groups]
     return pl.pallas_call(
         functools.partial(series_kernel, n_low, n_high, chunks),
-        in_specs=[*[pl.BlockSpec(memory_space=pltpu.SMEM)] * 2, *[vmem] * 3, *[hbm] * 3],
+        in_specs=[*[pl.BlockSpec(memory_space=pltpu.SMEM)] * 2, hbm, vmem, *[hbm] * 3],
         out_specs=(hbm, hbm),
         out_shape=(
             jax.ShapeDtypeStruct((n_sta, n_beams, n_sub, 2, rows_out, 128), jnp.int16),
@@ -473,8 +535,8 @@
             *per_side(lambda g, r: pltpu.VMEM((2, r * 2 * n_beams * pitch, 128), jnp.float32)),
             *per_side(lambda g, r: pltpu.VMEM((r - 1, n_beams, 2, 2, half, 128), jnp.int16)),
             *per_side(lambda g, r: pltpu.VMEM((r - 1, n_beams, 2, 2, half, 128), jnp.int16)),
-            *per_side(lambda g, r: pltpu.VMEM((r - 1, n_beams, 8, 128), jnp.float32)),
-            *per_side(lambda g, r: pltpu.VMEM((r - 1, n_beams, 8, 128), jnp.float32)),
+            *per_side(lambda g, r: pltpu.VMEM((r - 1, n_beams, 2, 8, 128), jnp.float32)),
+            *per_side(lambda g, r: pltpu.VMEM((r - 1, n_beams, 2, 8, 128), jnp.float32)),
             *per_side(lambda g, r: dma((g - 1,))),
             *per_side(lambda g, r: dma((g - 1, chunks))),
             *per_side(lambda g, r: dma((r - 1,))),
@@ -503,6 +565,8 @@
             pltpu.VMEM((2, weights.shape[1], 128), jnp.float32),
             *[pltpu.VMEM(table.shape, table.dtype) for table in tables],
             dma((3,)),
+            pltpu.VMEM(volts.shape, volts.dtype),
+            dma((4,)),
         ],
         compiler_params=pltpu.CompilerParams(
             collective_id=0, has_side_effects=True, vmem_limit_bytes=60 * 1024 * 1024
@@ -510,7 +574,7 @@
         cost_estimate=pl.CostEstimate(
             flops=8 * n_beams * depth * blocks * 128, bytes_accessed=2 * volts.size, transcendentals=0
         ),
-    )(dm_index[:, 0], delays, volts, weights, base_phase, *tables)
+    )(dm_index[:, 0], delays, volts, weights, *tables)
 
 
 def unpack_kernel(codes_ref, peak_ref, out_ref, power_ref):
@@ -556,10 +620,8 @@
     assert sub_dev == 1 and trials == 1 and root_len * root_len == total_len
     n_low = 2 if n_sta % 2 == 0 else 1
     n_high = n_sta // n_low
-    subband = lax.axis_index("sub") + jnp.arange(1, dtype=jnp.int32)
-    base_phase = chirp_base(subband, root_len, total_len)
     codes, peak = make_series(
-        dm_index, station_delays, voltages[0], beam_weights[0], base_phase, n_low, n_high, n_sub, root_len
+        dm_index, station_delays, voltages[0], beam_weights[0], n_low, n_high, n_sub, root_len
     )
     moved, intensity = unpack_series(codes, peak)
     return (moved.reshape(*moved.shape[:3], 1, -1), intensity.reshape(intensity.shape[0], 1, -1))

time: 123 us -> 120 us (0.976)
  Pallas kernels: 122 us -> 119 us
    pallas_call x1, Pallas kernels: 117 us -> 114 us  [make_series(): pl.pallas_call(functools.partial(series_kernel, n_low, n_high, chunks), i...]
where the time goes in v5:
time: 120 us; the launch traced here: 119 us
  Pallas kernels  119 us (99%)
    pallas_call x1, Pallas kernels, make_series(): pl.pallas_call(functools.partial(series_kernel, n_low, n_high, chunks), i...  114 us
    pallas_call x1, Pallas kernels, unpack_series(): pl.pallas_call(unpack_kernel, grid=(n_sta,), in_specs=[pl.BlockSpec((1, n...  4.47 us

profile of v5, /device:TPU:0, one launch (start us, length us, event | category | flops | bytes accessed | tf_op | source)
XLA Modules:
  0.0 119.4 jit_solution(8231788397936468)
XLA Ops:
  0.6 114.2 %shard_map.86 = (s16[4,8,8,2,16,128]{5,4,3,2,1,0:T(8,128)(2,1)}, f32[4,8,8,128]{3,2,1,0:T(8,128)}) custom-call(s32[8]{0:T(128)} %bitcast.7, s32[16]{0:T(128)} %delay_ref.1, bf16[2,16,65536]{2,1,0:T(8,128)(2,1)} %bitcast.5, bf16[2,32,64]{2,1,0:T(8,128)(2,1)} %bitcast.6, bf16[2,512,512]{2,1,0:T(8,128)(2,1)} %constant.6.clone.left_hbm, ...), custom_call_target="tpu_custom_call" | custom-call | flops 134217728 | bytes 4194304 | tf_op jit(solution)/shard_map/pallas_call | solution.py:525
  114.9 4.5 %shard_map.87 = (f32[8,2,32,16,128]{4,3,2,1,0:T(8,128)}, f32[32,16,128]{2,1,0:T(8,128)}) custom-call(s16[4,8,8,2,16,128]{5,4,3,2,1,0:T(8,128)(2,1)} %get-tuple-element.6.codes_ref, f32[4,8,8,128]{3,2,1,0:T(8,128)} %get-tuple-element.7.peak_ref), custom_call_target="tpu_custom_call" | custom-call | tf_op jit(solution)/shard_map/pallas_call | solution.py:594

commit v6 on v5

--- a/solution.py
+++ b/solution.py
@@ -429,6 +429,15 @@
 
     def keep(beam):
         return pltpu.make_async_copy(middle.at[beam, :, sta], out_ref.at[sta, beam], own_sem.at[0])
+
+    lag = 5
+
+    def spread(beam, carry):
+        total_of(middle.at[beam, pl.ds(0, n_sub - 1)], move_send.at[0], move_recv.at[beam]).wait_recv()
+        for k in range(1, n_sta):
+            forward(beam, k).start()
+        keep(beam).start()
+        return carry
 
     def finish(beam, carry):
         for side in range(2):
@@ -466,6 +475,11 @@
         middle[beam, sub] = ready[sub, beam]
         for k in range(1, n_sub):
             move(beam, k).start()
+
+        @pl.when(beam >= lag)
+        def _():
+            spread(beam - lag, 0)
+
         return carry
 
     lax.fori_loop(0, n_beams, finish, 0)
@@ -473,14 +487,7 @@
     for k in range(1, n_sub):
         move_peak(k).start()
 
-    def spread(beam, carry):
-        total_of(middle.at[beam, pl.ds(0, n_sub - 1)], move_send.at[0], move_recv.at[beam]).wait_recv()
-        for k in range(1, n_sta):
-            forward(beam, k).start()
-        keep(beam).start()
-        return carry
-
-    lax.fori_loop(0, n_beams, spread, 0)
+    lax.fori_loop(max(n_beams - lag, 0), n_beams, spread, 0)
     arrived = middle_peak.at[pl.ds(0, n_sub - 1)]
     total_of(arrived, peak_send, peak_recv).wait_recv()
     for k in range(1, n_sta):
@@ -579,28 +586,32 @@
 
 def unpack_kernel(codes_ref, peak_ref, out_ref, power_ref):
     n_sub, _, n_beams = out_ref.shape[:3]
-    for beam in range(n_beams):
-        power = jnp.zeros(power_ref.shape[1:], jnp.float32)
-        for sub in range(n_sub):
-            for part in range(2):
-                values = dequantize(codes_ref[0, beam, sub, part], peak_ref[0, sub, beam : beam + 1, :])
-                out_ref[sub, part, beam] = values
-                power = power + values * values
-        power_ref[beam] = power * (1.0 / n_sub)
+    for owner in range(codes_ref.shape[0]):
+        for beam in range(codes_ref.shape[1]):
+            at = owner * codes_ref.shape[1] + beam
+            power = jnp.zeros(power_ref.shape[1:], jnp.float32)
+            for sub in range(n_sub):
+                ceiling = peak_ref[owner, sub, beam : beam + 1, :]
+                for part in range(2):
+                    values = dequantize(codes_ref[owner, beam, sub, part], ceiling)
+                    out_ref[sub, part, at] = values
+                    power = power + values * values
+            power_ref[at] = power * (1.0 / n_sub)
 
 
 def unpack_series(codes, peak):
     n_sta, n_beams, n_sub, _, rows, lanes = codes.shape
+    group = n_sta // 2
     return pl.pallas_call(
         unpack_kernel,
-        grid=(n_sta,),
+        grid=(n_sta // group,),
         in_specs=[
-            pl.BlockSpec((1, n_beams, n_sub, 2, rows, lanes), lambda i: (i, 0, 0, 0, 0, 0)),
-            pl.BlockSpec((1, n_sub, n_beams, lanes), lambda i: (i, 0, 0, 0)),
+            pl.BlockSpec((group, n_beams, n_sub, 2, rows, lanes), lambda i: (i, 0, 0, 0, 0, 0)),
+            pl.BlockSpec((group, n_sub, n_beams, lanes), lambda i: (i, 0, 0, 0)),
         ],
         out_specs=[
-            pl.BlockSpec((n_sub, 2, n_beams, rows, lanes), lambda i: (0, 0, i, 0, 0)),
-            pl.BlockSpec((n_beams, rows, lanes), lambda i: (i, 0, 0)),
+            pl.BlockSpec((n_sub, 2, group * n_beams, rows, lanes), lambda i: (0, 0, i, 0, 0)),
+            pl.BlockSpec((group * n_beams, rows, lanes), lambda i: (i, 0, 0)),
         ],
         out_shape=[
             jax.ShapeDtypeStruct((n_sub, 2, n_sta * n_beams, rows, lanes), jnp.float32),

time: 120 us -> 119 us (level)
  no operation moved by 1% of the time
where the time goes in v6:
time: 119 us
  Pallas kernels  118 us (99%)
    pallas_call x1, Pallas kernels, make_series(): pl.pallas_call(functools.partial(series_kernel, n_low, n_high, chunks), i...  114 us
    pallas_call x1, Pallas kernels, unpack_series(): pl.pallas_call(unpack_kernel, grid=(n_sta // group,), in_specs=[pl.BlockS...  3.69 us

profile of v6, /device:TPU:0, one launch (start us, length us, event | category | flops | bytes accessed | tf_op | source)
XLA Modules:
  0.0 118.6 jit_solution(586263688047376827)
XLA Ops:
  0.6 114.2 %shard_map.86 = (s16[4,8,8,2,16,128]{5,4,3,2,1,0:T(8,128)(2,1)}, f32[4,8,8,128]{3,2,1,0:T(8,128)}) custom-call(s32[8]{0:T(128)} %bitcast.7, s32[16]{0:T(128)} %delay_ref.1, bf16[2,16,65536]{2,1,0:T(8,128)(2,1)} %bitcast.5, bf16[2,32,64]{2,1,0:T(8,128)(2,1)} %bitcast.6, bf16[2,512,512]{2,1,0:T(8,128)(2,1)} %constant.6.clone.left_hbm, ...), custom_call_target="tpu_custom_call" | custom-call | flops 134217728 | bytes 4194304 | tf_op jit(solution)/shard_map/pallas_call | solution.py:532
  114.9 3.7 %shard_map.87 = (f32[8,2,32,16,128]{4,3,2,1,0:T(8,128)}, f32[32,16,128]{2,1,0:T(8,128)}) custom-call(s16[4,8,8,2,16,128]{5,4,3,2,1,0:T(8,128)(2,1)} %get-tuple-element.6.codes_ref, f32[4,8,8,128]{3,2,1,0:T(8,128)} %get-tuple-element.7.peak_ref), custom_call_target="tpu_custom_call" | custom-call | tf_op jit(solution)/shard_map/pallas_call | solution.py:605

commit v7 on v6

--- a/solution.py
+++ b/solution.py
@@ -47,8 +47,9 @@
 
 
 def dot3(a_high, a_low, b_high, b_low):
-    dot = functools.partial(jnp.dot, preferred_element_type=jnp.float32)
-    return dot(a_high, b_high) + (dot(a_high, b_low) + dot(a_low, b_high))
+    left = jnp.concatenate([a_high, a_high, a_low], axis=1)
+    right = jnp.concatenate([b_high, b_low, b_high], axis=0)
+    return jnp.dot(left, right, preferred_element_type=jnp.float32)
 
 
 MESH = pl.DeviceIdType.MESH

time: 119 us -> 119 us (level)
  no operation moved by 1% of the time
where the time goes in v7:
time: 119 us
  Pallas kernels  118 us (99%)
    pallas_call x1, Pallas kernels, make_series(): pl.pallas_call(functools.partial(series_kernel, n_low, n_high, chunks), i...  114 us
    pallas_call x1, Pallas kernels, unpack_series(): pl.pallas_call(unpack_kernel, grid=(n_sta // group,), in_specs=[pl.BlockS...  3.69 us

profile of v7, /device:TPU:0, one launch (start us, length us, event | category | flops | bytes accessed | tf_op | source)
XLA Modules:
  0.0 118.6 jit_solution(4433747141268587624)
XLA Ops:
  0.6 114.2 %shard_map.86 = (s16[4,8,8,2,16,128]{5,4,3,2,1,0:T(8,128)(2,1)}, f32[4,8,8,128]{3,2,1,0:T(8,128)}) custom-call(s32[8]{0:T(128)} %bitcast.7, s32[16]{0:T(128)} %delay_ref.1, bf16[2,16,65536]{2,1,0:T(8,128)(2,1)} %bitcast.5, bf16[2,32,64]{2,1,0:T(8,128)(2,1)} %bitcast.6, bf16[2,512,512]{2,1,0:T(8,128)(2,1)} %constant.6.clone.left_hbm, ...), custom_call_target="tpu_custom_call" | custom-call | flops 134217728 | bytes 4194304 | tf_op jit(solution)/shard_map/pallas_call | solution.py:533
  114.9 3.7 %shard_map.87 = (f32[8,2,32,16,128]{4,3,2,1,0:T(8,128)}, f32[32,16,128]{2,1,0:T(8,128)}) custom-call(s16[4,8,8,2,16,128]{5,4,3,2,1,0:T(8,128)(2,1)} %get-tuple-element.6.codes_ref, f32[4,8,8,128]{3,2,1,0:T(8,128)} %get-tuple-element.7.peak_ref), custom_call_target="tpu_custom_call" | custom-call | tf_op jit(solution)/shard_map/pallas_call | solution.py:606
